TPU v7x, 256 devices: a 8x8x2 block of a 8x8x16 slice. The times are simulated.
256 devices in a mesh: groups: 2 (over z), band: 64 (over y, x), sub: 2 (over core).
Axes of the slice: x: 8, y: 8, z: 2, core: 2. Of those that a mesh axis runs over, the one named last changes fastest.
The devices are a block of a 8x8x16 slice.
Arguments:
- sky_maps: bfloat16 [256, 2, 32, 16384], P(('groups', 'band', 'sub')), parts along dimension 0, may hold values from -6 to 6
- sky_mask: float32 [256, 16384], P(('groups', 'band', 'sub')), parts along dimension 0, may hold values from 0.005 to 1, as said below
- pixel_counts: int32 [256], P(('groups', 'band', 'sub')), parts along dimension 0, may hold values from 8192 to 16384, as said below
- phi_offsets: int32 [256], P(('groups', 'band', 'sub')), parts along dimension 0, may hold values from 0 to 1
- low_orders: int32 [256], P('groups'), parts along dimension 0, may hold values from 1 to 4095, as said below
- legendre: bfloat16 [256, 8192, 256], P(('groups', 'band', 'sub')), parts along dimension 0, may hold values from -0.375 to 0.375
Outputs:
- alm_packed: float32 [256, 8192, 128], P(('groups', 'band', 'sub')), parts along dimension 0
- spectra: float32 [16384, 2, 1024], P(('groups', 'band', 'sub')), parts along dimension 0
There are 2 independent parts, one for each index of `groups`. A program takes and returns all parts, laid end to end along the dimension named above; each array names one. Nothing has to cross between parts.
Inputs may be any that keep to these rules, and one draw needn't show every extreme that they name: `pixel_counts`: multiples of 4; some cycle has exactly 16384 pixels; pixel slots at or past a cycle's count are not used. `low_orders`: all distinct. `sky_mask`: Positive.
All inputs are finite; a program needn't handle non-finite values.
Results may differ from a plain program's by a relative error of at most 0.0046.
Values may be sent and summed in bfloat16 or wider, within the bound.
No kernel may reach another device: no remote copies, remote signals or barrier semaphores. Data moves between devices by JAX's collectives and lax.ppermute only.
A program may use at most 64 MiB of HBM per device.

v0:
```python
import functools

import jax
import jax.numpy as jnp
from jax import lax
from jax.sharding import Mesh
from jax.sharding import PartitionSpec as P

BAND_SUB = ("band_0", "band_1", "sub")
BAND = ("band_0", "band_1")
GROUPS_BAND_SUB = ("groups", "band_0", "band_1", "sub")


def by_axis(array, axes):
    return functools.reduce(lax.psum, axes, array)


def cut_along(array, dim, devices):
    shape = array.shape
    tiles = array.reshape(*shape[:dim], devices, shape[dim] // devices, *shape[dim + 1 :])
    return jnp.moveaxis(tiles, dim, 0)


def in_order(tiles, dim):
    tiles = jnp.moveaxis(tiles, 0, dim)
    shape = tiles.shape
    return tiles.reshape(*shape[:dim], shape[dim] * shape[dim + 1], *shape[dim + 2 :])


def one_exchange(array, axis, axes, splits, concats):
    sizes = [lax.axis_size(a) for a in axes]
    tiles = cut_along(array, splits[0], sizes[0])
    tiles = jnp.moveaxis(cut_along(tiles, splits[1] + 1, sizes[1]), 0, 1)
    inside = tiles.shape[2:]
    tiles = tiles.reshape(-1, *inside)
    tiles = lax.all_to_all(tiles, axis, split_axis=0, concat_axis=0, tiled=True)
    tiles = in_order(tiles.reshape(*sizes, *inside), concats[0] + 1)
    return in_order(tiles, concats[1])


def from_partner(block, axis, stride):
    count = lax.axis_size(axis)
    route = []
    for low in range(count):
        high = low | 1 << stride
        if high != low and high < count:
            route += [(low, high), (high, low)]
    return lax.ppermute(block, axis, route)


def slot_orders(low_orders, degree_count):
    return jnp.stack([low_orders, degree_count - low_orders], axis=1).reshape(-1)


def finish_cycle(pixel_sums, cycle_count, orders):
    slots = orders.shape[0]
    maps_count = pixel_sums.shape[1] // 2
    inverse_root = 1.0 / jnp.sqrt(cycle_count.astype(jnp.float32))
    real_part = (pixel_sums[:slots] * inverse_root).reshape(slots, 2, maps_count)
    imag_part = (-pixel_sums[slots:] * inverse_root).reshape(slots, 2, maps_count)
    joined = jnp.stack(
        [real_part[:, 0], imag_part[:, 0], real_part[:, 1], imag_part[:, 1]], axis=1
    ).reshape(slots, 4 * maps_count)
    live_slots = 2 * orders < cycle_count
    return jnp.where(live_slots[:, None], joined, 0.0).astype(jnp.bfloat16)


def cycle_fourier(cycle_maps, cycle_mask, cycle_count, cycle_offset, orders):
    maps_count = cycle_maps.shape[1]
    pixel_slots = cycle_maps.shape[2]
    cycle_rows = cycle_maps.reshape(2 * maps_count, pixel_slots)
    block_width = min(2048, pixel_slots)
    group_count = block_width // 128
    slots = orders.shape[0]
    modulus = 2 * cycle_count
    scale = jnp.pi / cycle_count.astype(jnp.float32)
    order_mod = orders % modulus
    fine_units = 2 * order_mod[:, None] * jnp.arange(128, dtype=jnp.int32)[None, :] % modulus
    fine_angle = scale * fine_units.astype(jnp.float32)
    fine_cos = jnp.cos(fine_angle)[:, None, :]
    fine_sin = jnp.sin(fine_angle)[:, None, :]

    def add_block(block_index, totals):
        first_pixel = block_index * block_width
        row_block = lax.dynamic_slice_in_dim(cycle_rows, first_pixel, block_width, 1)
        mask_block = lax.dynamic_slice_in_dim(cycle_mask, first_pixel, block_width, 0)
        pixels = first_pixel + jnp.arange(block_width, dtype=jnp.int32)
        masked = jnp.where(
            pixels[None, :] < cycle_count, mask_block[None, :] * row_block.astype(jnp.float32), 0.0
        ).astype(jnp.bfloat16)
        group_starts = first_pixel + 128 * jnp.arange(group_count, dtype=jnp.int32)
        coarse_units = (
            order_mod[:, None] * ((2 * group_starts[None, :] + cycle_offset) % modulus) % modulus
        )
        coarse_angle = scale * coarse_units.astype(jnp.float32)
        coarse_cos = jnp.cos(coarse_angle)[:, :, None]
        coarse_sin = jnp.sin(coarse_angle)[:, :, None]
        cosines = (coarse_cos * fine_cos - coarse_sin * fine_sin).reshape(slots, block_width)
        sines = (coarse_sin * fine_cos + coarse_cos * fine_sin).reshape(slots, block_width)
        tables = jnp.concatenate([cosines.astype(jnp.bfloat16), sines.astype(jnp.bfloat16)], axis=0)
        return totals + lax.dot_general(
            tables, masked, (((1,), (1,)), ((), ())), preferred_element_type=jnp.float32
        )

    block_count = (cycle_count + block_width - 1) // block_width
    pixel_sums = lax.fori_loop(
        0, block_count, add_block, jnp.zeros((2 * slots, 2 * maps_count), jnp.float32)
    )
    return finish_cycle(pixel_sums, cycle_count, orders)


def stacked_operand(block_rows):
    quarter = block_rows.shape[1] // 4
    q_real = block_rows[:, :quarter]
    q_imag = block_rows[:, quarter : 2 * quarter]
    u_real = block_rows[:, 2 * quarter : 3 * quarter]
    u_imag = block_rows[:, 3 * quarter :]
    lower_half = jnp.concatenate([u_imag, -u_real, -q_imag, q_real], axis=1)
    return jnp.concatenate([block_rows, lower_half], axis=0)


def pair_alm(legendre_rows, first_order, first_block, second_block):
    first_operand = stacked_operand(first_block)
    second_operand = stacked_operand(second_block)
    degree_count, inner_width = legendre_rows.shape
    tile_height = min(128, degree_count)
    tile_count = degree_count // tile_height
    split_row = degree_count - first_order
    tile_starts = jnp.arange(tile_count, dtype=jnp.int32) * tile_height
    chosen = jnp.where(
        (tile_starts < split_row)[:, None, None], first_operand[None], second_operand[None]
    )
    tile_product = jnp.einsum(
        "tir,tro->tio",
        legendre_rows.reshape(tile_count, tile_height, inner_width),
        chosen,
        preferred_element_type=jnp.float32,
    )
    tile_product = tile_product.reshape(degree_count, first_operand.shape[1])
    border = split_row // tile_height * tile_height
    border_rows = lax.dynamic_slice_in_dim(legendre_rows, border, tile_height, 0)
    border_product = jnp.dot(border_rows, second_operand, preferred_element_type=jnp.float32)
    current = lax.dynamic_slice_in_dim(tile_product, border, tile_height, 0)
    row_index = border + jnp.arange(tile_height, dtype=jnp.int32)
    patched = jnp.where((row_index >= split_row)[:, None], border_product, current)
    return -lax.dynamic_update_slice_in_dim(tile_product, patched, border, 0)


def outer_totals(rows, maps_count):
    split_parts = rows.reshape(rows.shape[0], rows.shape[1], 2, 2, maps_count)
    return jnp.einsum(
        "slerm,slern->lemn", split_parts, split_parts, preferred_element_type=jnp.float32
    )


def scaled_spectra(totals, degrees, orders, weight, maps_count):
    counts = jnp.maximum(
        jnp.sum((orders[None, :] <= degrees[:, None]).astype(jnp.int32), axis=1), 1
    ).astype(jnp.float32)
    return (2.0 * totals / (weight * counts)[:, None, None, None]).reshape(
        degrees.shape[0], 2, maps_count * maps_count
    )


def low_positions(device_ids, devices, range_rows):
    half_rows = range_rows // 2
    pair_block = jnp.minimum(device_ids, devices - 1 - device_ids)
    upper_flag = (device_ids >= devices // 2).astype(jnp.int32)
    return (
        pair_block[:, None] * range_rows
        + upper_flag[:, None] * half_rows
        + jnp.arange(half_rows, dtype=jnp.int32)[None, :]
    )


def local(sky_maps, sky_mask, pixel_counts, phi_offsets, low_orders, legendre):
    devices = lax.axis_size(BAND_SUB)
    device_index = lax.axis_index(BAND_SUB)
    degree_count = legendre.shape[1]
    orders = slot_orders(low_orders, degree_count)
    cycle_local = sky_maps.shape[0]
    maps_count = sky_maps.shape[2]
    pair_local = legendre.shape[0]
    slot_local = 2 * pair_local
    columns = 4 * maps_count
    valid_pixels = jnp.arange(sky_maps.shape[3], dtype=jnp.int32)[None, :] < pixel_counts[:, None]
    local_square = jnp.sum(jnp.where(valid_pixels, sky_mask * sky_mask, 0.0))
    local_pixels = jnp.sum(pixel_counts.astype(jnp.float32))
    total_square, total_pixels = (by_axis(local_square, BAND_SUB), by_axis(local_pixels, BAND_SUB))
    weight = total_square / total_pixels
    cycle_blocks = [
        cycle_fourier(sky_maps[0], sky_mask[0], pixel_counts[0], phi_offsets[0], orders)
    ]
    coefficients = jnp.stack(cycle_blocks, axis=1).reshape(
        devices, slot_local, cycle_local, columns
    )
    band_count = lax.axis_size(BAND)
    sectioned = coefficients.reshape(
        band_count, devices // band_count, slot_local, cycle_local, columns
    )
    received = one_exchange(sectioned, BAND_SUB, (BAND, "sub"), (0, 1), (0, 1))
    received = received.reshape(devices, slot_local, cycle_local, columns)
    cycle_total = devices * cycle_local
    pair_index = 0
    first_order = lax.dynamic_index_in_dim(
        low_orders, device_index * pair_local + pair_index, 0, keepdims=False
    )
    first_block = received[:, 2 * pair_index].reshape(cycle_total, columns)
    second_block = received[:, 2 * pair_index + 1].reshape(cycle_total, columns)
    alm_pairs = [pair_alm(legendre[pair_index], first_order, first_block, second_block)]
    first_orders = [first_order]
    alm_packed = jnp.stack(alm_pairs, axis=0)
    range_rows = degree_count // devices
    half_rows = range_rows // 2
    all_devices = jnp.arange(devices, dtype=jnp.int32)
    dest_low = low_positions(all_devices, devices, range_rows)
    outgoing = []
    pair_index = 0
    first_order = first_orders[pair_index]
    packed_rows = alm_pairs[pair_index].astype(jnp.bfloat16)
    index_low = jnp.where(
        dest_low >= first_order, dest_low - first_order, degree_count - 1 - dest_low
    )
    index_mirror = degree_count - 1 - dest_low - first_order
    row_table = jnp.concatenate([index_low, index_mirror], axis=1).reshape(-1)
    outgoing.append(jnp.take(packed_rows, row_table, axis=0).reshape(devices, range_rows, columns))
    outgoing = jnp.stack(outgoing, axis=1)
    incoming = lax.all_to_all(outgoing, BAND_SUB, split_axis=0, concat_axis=0, tiled=True)
    incoming = incoming.reshape(devices * pair_local, range_rows, columns)
    own_low = low_positions(device_index[None], devices, range_rows)[0]
    own_mirror = degree_count - 1 - own_low
    kept_mask = own_low[None, :] >= low_orders[:, None]
    low_rows = incoming[:, :half_rows]
    mirror_rows = incoming[:, half_rows:]
    low_kept = jnp.where(kept_mask[:, :, None], low_rows, jnp.zeros_like(low_rows))
    low_moved = jnp.where(kept_mask[:, :, None], jnp.zeros_like(low_rows), low_rows)
    low_totals = outer_totals(low_kept, maps_count)
    mirror_totals = outer_totals(mirror_rows, maps_count) + outer_totals(low_moved, maps_count)
    low_spectra = scaled_spectra(low_totals, own_low, orders, weight, maps_count)
    mirror_spectra = jnp.flip(
        scaled_spectra(mirror_totals, own_mirror, orders, weight, maps_count), axis=0
    )
    upper_device = device_index >= devices // 2
    swapped = jnp.where(upper_device, low_spectra, mirror_spectra)
    bit_count = devices.bit_length() - 1
    for bit in range(bit_count):
        swapped = from_partner(swapped.astype(jnp.bfloat16), BAND_SUB, bit).astype(swapped.dtype)
    spectra = jnp.where(
        upper_device,
        jnp.concatenate([mirror_spectra, swapped], axis=0),
        jnp.concatenate([low_spectra, swapped], axis=0),
    )
    return (alm_packed, spectra)


def solution(mesh):
    torus = Mesh(
        mesh.devices.reshape(mesh.shape["groups"], 8, 8, mesh.shape["sub"]),
        ("groups", "band_0", "band_1", "sub"),
    )
    in_specs = (
        P(GROUPS_BAND_SUB, None, None, None),
        P(GROUPS_BAND_SUB, None),
        P(GROUPS_BAND_SUB),
        P(GROUPS_BAND_SUB),
        P("groups"),
        P(GROUPS_BAND_SUB, None, None),
    )
    out_specs = (P(GROUPS_BAND_SUB, None, None), P(GROUPS_BAND_SUB, None, None))
    return jax.shard_map(local, mesh=torus, in_specs=in_specs, out_specs=out_specs, check_vma=False)
```

profile of v0, /device:TPU:518, one launch (start us, length us, event | category | flops | bytes accessed | tf_op | source)
XLA Modules:
  0.0 298.6 jit_solution(7764638201738838396)
XLA Ops:
  2.0 0.7 pad_add_fusion.1
  3.1 64.2 %while.14 = (s32[]{:T(128)}, f32[512,64]{0,1:T(8,128)S(1)}, s32[]{:T(128)}, f32[]{:T(128)}, s32[256]{0:T(256)S(1)}, /*index=5*/s32[]{:T(128)}, s32[]{:T(128)}, p...) while((s32[]{:T(128)}, f32[512,64]{0,1:T(8,128)S(1)}, ...), condition=%wide.region_1.2_spmd.clone.clone, body=%wide.region_0.1_spmd.clone.clone.sunk | while | flops 143536304 | bytes 9599346 | solution.py:106
  3.2 0.8 and_select_fusion.4
  4.5 1.8 cosine_bitcast_fusion.2
  6.3 2.4 subtract_convert_fusion.2
  9.2 0.7 dynamic_slice.42
  10.6 1.7 fusion.72
  12.3 0.8 and_select_fusion.4
  13.7 1.8 cosine_bitcast_fusion.2
  15.5 2.4 subtract_convert_fusion.2
  18.4 0.7 dynamic_slice.42
  19.8 1.7 fusion.72
  21.5 0.8 and_select_fusion.4
  22.9 1.8 cosine_bitcast_fusion.2
  24.7 2.4 subtract_convert_fusion.2
  27.6 0.7 dynamic_slice.42
  28.9 1.7 fusion.72
  30.7 0.8 and_select_fusion.4
  32.0 1.8 cosine_bitcast_fusion.2
  33.9 2.4 subtract_convert_fusion.2
  36.8 0.7 dynamic_slice.42
  38.1 1.7 fusion.72
  39.9 0.8 and_select_fusion.4
  41.2 1.8 cosine_bitcast_fusion.2
  43.0 2.4 subtract_convert_fusion.2
  45.9 0.7 dynamic_slice.42
  47.3 1.7 fusion.72
  49.0 0.8 and_select_fusion.4
  50.4 1.8 cosine_bitcast_fusion.2
  52.2 2.4 subtract_convert_fusion.2
  55.1 0.7 dynamic_slice.42
  56.5 1.7 fusion.72
  58.2 0.8 and_select_fusion.4
  59.6 1.8 cosine_bitcast_fusion.2
  61.4 2.4 subtract_convert_fusion.2
  64.3 0.7 dynamic_slice.42
  65.6 1.7 fusion.72
  68.0 0.8 fusion.44
  68.8 30.3 %all-to-all-start = ((bf16[128,1,1,2,1,128]{5,3,4,2,1,0:T(2,128)(2,1)}), bf16[128,1,1,2,1,128]{5,3,4,2,1,0:T(2,128)(2,1)S(1)}, u32[]{:S(2)}, u32[]{:S(2)}) async-start(bf16[128,1,1,2,1,128]{5,3,4,2,1,0:T(2,128)(2,1)} %fusion.44), calls=%async_computation | async-start | bytes 131072 | tf_op jit(solution)/shard_map/all_to_all | solution.py:36
  100.4 0.7 subtract_select_fusion
  101.5 7.3 %all-to-all-done = bf16[128,1,1,2,1,128]{5,3,4,2,1,0:T(2,128)(2,1)S(1)} async-done(((bf16[128,1,1,2,1,128]{5,3,4,2,1,0:T(2,128)(2,1)}), bf16[128,1,1,2,1,128]{5,3,4,2,1,0:T(2,128)(2,1)S(1)}, u32[]{:S(2)}, u32[]{:S(2)}) %all-to-all-start) | async-done | bytes 65568 | tf_op jit(solution)/shard_map/all_to_all | solution.py:36
  109.3 3.5 %fusion.32 = f32[64,128,128]{1,2,0:T(8,128)S(1)} fusion(bf16[64,128,256]{2,1,0:T(8,128)(2,1)} %bitcast.121, pred[64]{0:T(512)(128)(4,1)S(1)} %multiply_compare_fusion.1, bf16[256,128]{1,0:T(8,128)(2,1)S(1)} %maximum_maximum_fusion.1, bf16[256,128]{1,0:T(8,128)(2,1)S(1)} %maximum_maximum_fusion), kind=kOutput, calls=%fused_computation.42 | convolution fusion | flops 538968064 | bytes 8519744 | tf_op jit(solution)/shard_map/tir,tro->tio/dot_general | solution.py:133
  112.9 1.0 fusion.42
  113.9 2.6 negate_convert_fusion
  116.4 29.2 %gather_fusion = bf16[8192,128]{1,0:T(8,128)(2,1)} fusion(bf16[8192,128]{1,0:T(8,128)(2,1)S(1)} %get-tuple-element.277, s32[8192]{0:T(1024)S(1)} %broadcast_clamp_fusion), kind=kCustom, calls=%fused_computation | custom fusion | bytes 4227072 | tf_op jit(solution)/shard_map/jit(_take)/gather | solution.py:226
  145.6 4.4 %broadcast_select_fusion = bf16[128,1,64,128]{3,2,1,0:T(8,128)(2,1)} fusion(bf16[128,1,64,128]{3,2,1,0:T(8,128)(2,1)} %bitcast.104, pred[128,64]{1,0:T(8,128)(4,1)S(1)} %get-tuple-element.265), kind=kLoop, calls=%fused_computation.49 | loop fusion | flops 1048576 | bytes 4202496 | tf_op jit(solution)/shard_map/jit(_take)/select_n | solution.py:226
  150.1 10.2 %all-to-all-start.1 = ((bf16[128,1,64,128]{3,2,1,0:T(8,128)(2,1)}), bf16[128,1,64,128]{3,2,1,0:T(8,128)(2,1)S(1)}, u32[]{:S(2)}, u32[]{:S(2)}) async-start(bf16[128,1,64,128]{3,2,1,0:T(8,128)(2,1)} %broadcast_select_fusion), calls=%async_computation.1 | async-start | bytes 4194304 | tf_op jit(solution)/shard_map/all_to_all | solution.py:228
  160.3 0.7 fusion.50
  161.0 55.5 %all-reduce.1 = (f32[]{:T(128)}, f32[]{:T(128)}) all-reduce(f32[]{:T(128)} %fusion.50, f32[]{:T(128)} %bitcast.39), channel_id=1, replica_groups=mesh['groups'=2,'band_0'=8,'band_1'=8,'sub'=2] {'band_0'}, use_global_device_ids=true, to_apply=%region_3.4 | all-reduce | flops 2 | bytes 16 | tf_op jit(solution)/shard_map/psum | solution.py:15
  216.5 17.1 %all-reduce = (f32[]{:T(128)}, f32[]{:T(128)}) all-reduce(f32[]{:T(128)} %get-tuple-element.261, f32[]{:T(128)} %get-tuple-element.262), channel_id=1, replica_groups=mesh['groups'=2,'band_0'=8,'band_1'=8,'sub'=2] {'band_1'}, use_global_device_ids=true, to_apply=%region_4.5 | all-reduce | flops 2 | bytes 16 | tf_op jit(solution)/shard_map/psum | solution.py:15
  233.6 3.2 %all-reduce.2 = (f32[]{:T(128)}, f32[]{:T(128)}) all-reduce(f32[]{:T(128)} %get-tuple-element.259, f32[]{:T(128)} %get-tuple-element.260), channel_id=1, replica_groups=mesh['groups'=2,'band_0'=8,'band_1'=8,'sub'=2] {'sub'}, use_global_device_ids=true, to_apply=%region_5.6 | all-reduce | flops 2 | bytes 16 | tf_op jit(solution)/shard_map/psum | solution.py:15
  238.4 3.0 copy.58
  241.4 1.7 broadcast_select_fusion.2
  246.0 1.2 collective-permute-done
  247.2 5.6 %collective-permute-done.1 = bf16[32,2,1024]{2,1,0:T(2,128)(2,1)S(1)} collective-permute-done((bf16[32,2,1024]{2,1,0:T(2,128)(2,1)S(1)}, bf16[32,2,1024]{2,1,0:T(2,128)(2,1)S(1)}, u32[]{:S(2)}, u32[]{:S(2)}) %collective-permute-start.1) | collective-permute-done | bytes 131104 | tf_op jit(solution)/shard_map/ppermute | solution.py:48
  253.0 8.2 %collective-permute-done.2 = bf16[32,2,1024]{2,1,0:T(2,128)(2,1)S(1)} collective-permute-done((bf16[32,2,1024]{2,1,0:T(2,128)(2,1)S(1)}, bf16[32,2,1024]{2,1,0:T(2,128)(2,1)S(1)}, u32[]{:S(2)}, u32[]{:S(2)}) %collective-permute-start.2) | collective-permute-done | bytes 131104 | tf_op jit(solution)/shard_map/ppermute | solution.py:48
  261.1 2.4 collective-permute-start.3
  263.5 8.8 %collective-permute-done.3 = bf16[32,2,1024]{2,1,0:T(2,128)(2,1)S(1)} collective-permute-done((bf16[32,2,1024]{2,1,0:T(2,128)(2,1)S(1)}, bf16[32,2,1024]{2,1,0:T(2,128)(2,1)S(1)}, u32[]{:S(2)}, u32[]{:S(2)}) %collective-permute-start.3) | collective-permute-done | bytes 131104 | tf_op jit(solution)/shard_map/ppermute | solution.py:48
  272.6 5.1 %collective-permute-done.4 = bf16[32,2,1024]{2,1,0:T(2,128)(2,1)S(1)} collective-permute-done((bf16[32,2,1024]{2,1,0:T(2,128)(2,1)S(1)}, bf16[32,2,1024]{2,1,0:T(2,128)(2,1)S(1)}, u32[]{:S(2)}, u32[]{:S(2)}) %collective-permute-start.4) | collective-permute-done | bytes 131104 | tf_op jit(solution)/shard_map/ppermute | solution.py:48
  277.7 1.3 collective-permute-start.5
  278.9 6.7 %collective-permute-done.5 = bf16[32,2,1024]{2,1,0:T(2,128)(2,1)S(1)} collective-permute-done((bf16[32,2,1024]{2,1,0:T(2,128)(2,1)S(1)}, bf16[32,2,1024]{2,1,0:T(2,128)(2,1)S(1)}, u32[]{:S(2)}, u32[]{:S(2)}) %collective-permute-start.5) | collective-permute-done | bytes 131104 | tf_op jit(solution)/shard_map/ppermute | solution.py:48
  285.6 4.9 %collective-permute-start.6 = (bf16[32,2,1024]{2,1,0:T(2,128)(2,1)S(1)}, bf16[32,2,1024]{2,1,0:T(2,128)(2,1)S(1)}, u32[]{:S(2)}, u32[]{:S(2)}) collective-permute-start(bf16[32,2,1024]{2,1,0:T(2,128)(2,1)S(1)} %collective-permute-done.5), channel_id=1, source_target_pairs={{0,64},{64,0},{1,65},{65,1},{2,66},{66,2},{3,67},{67,3},{4,68},{68... | collective-permute-start | bytes 393224 | tf_op jit(solution)/shard_map/ppermute | solution.py:48
  290.5 6.9 %collective-permute-done.6 = bf16[32,2,1024]{2,1,0:T(2,128)(2,1)S(1)} collective-permute-done((bf16[32,2,1024]{2,1,0:T(2,128)(2,1)S(1)}, bf16[32,2,1024]{2,1,0:T(2,128)(2,1)S(1)}, u32[]{:S(2)}, u32[]{:S(2)}) %collective-permute-start.6) | collective-permute-done | bytes 131104 | tf_op jit(solution)/shard_map/ppermute | solution.py:48
  297.5 1.1 fusion.43
  (84 shorter events, 18.7 us)
Async XLA Ops:
  3.1 64.7 %copy-start.1 = (s32[128]{0:T(128)S(1)}, s32[128]{0:T(128)}, u32[]{:S(2)}) copy-start(s32[128]{0:T(128)} %param.12) | copy-start | bytes 1540
  68.8 40.0 %all-to-all-start = ((bf16[128,1,1,2,1,128]{5,3,4,2,1,0:T(2,128)(2,1)}), bf16[128,1,1,2,1,128]{5,3,4,2,1,0:T(2,128)(2,1)S(1)}, u32[]{:S(2)}, u32[]{:S(2)}) async-start(bf16[128,1,1,2,1,128]{5,3,4,2,1,0:T(2,128)(2,1)} %fusion.44), calls=%async_computation | async-start | bytes 131072 | tf_op jit(solution)/shard_map/all_to_all | solution.py:36
  150.0 10.2 %copy-start = (f32[16384]{0:T(1024)S(1)}, f32[16384]{0:T(1024)}, u32[]{:S(2)}) copy-start(f32[16384]{0:T(1024)} %get-tuple-element.446) | copy-start | bytes 196612
  150.1 88.4 %all-to-all-start.1 = ((bf16[128,1,64,128]{3,2,1,0:T(8,128)(2,1)}), bf16[128,1,64,128]{3,2,1,0:T(8,128)(2,1)S(1)}, u32[]{:S(2)}, u32[]{:S(2)}) async-start(bf16[128,1,64,128]{3,2,1,0:T(8,128)(2,1)} %broadcast_select_fusion), calls=%async_computation.1 | async-start | bytes 4194304 | tf_op jit(solution)/shard_map/all_to_all | solution.py:228
  245.7 1.5 collective-permute-start
  247.2 5.6 %collective-permute-start.1 = (bf16[32,2,1024]{2,1,0:T(2,128)(2,1)S(1)}, bf16[32,2,1024]{2,1,0:T(2,128)(2,1)S(1)}, u32[]{:S(2)}, u32[]{:S(2)}) collective-permute-start(bf16[32,2,1024]{2,1,0:T(2,128)(2,1)S(1)} %collective-permute-done), channel_id=1, source_target_pairs={{0,2},{2,0},{1,3},{3,1},{4,6},{6,4},{5,7},{7,5},{8,10},{10,8},{9,1... | collective-permute-start | bytes 393224 | tf_op jit(solution)/shard_map/ppermute | solution.py:48
  252.7 8.4 %collective-permute-start.2 = (bf16[32,2,1024]{2,1,0:T(2,128)(2,1)S(1)}, bf16[32,2,1024]{2,1,0:T(2,128)(2,1)S(1)}, u32[]{:S(2)}, u32[]{:S(2)}) collective-permute-start(bf16[32,2,1024]{2,1,0:T(2,128)(2,1)S(1)} %collective-permute-done.1), channel_id=1, source_target_pairs={{0,4},{4,0},{1,5},{5,1},{2,6},{6,2},{3,7},{7,3},{8,12},{12,8},{9,1... | collective-permute-start | bytes 393224 | tf_op jit(solution)/shard_map/ppermute | solution.py:48
  261.1 11.1 %collective-permute-start.3 = (bf16[32,2,1024]{2,1,0:T(2,128)(2,1)S(1)}, bf16[32,2,1024]{2,1,0:T(2,128)(2,1)S(1)}, u32[]{:S(2)}, u32[]{:S(2)}) collective-permute-start(bf16[32,2,1024]{2,1,0:T(2,128)(2,1)S(1)} %collective-permute-done.2), channel_id=1, source_target_pairs={{0,8},{8,0},{1,9},{9,1},{2,10},{10,2},{3,11},{11,3},{4,12},{12,4},... | collective-permute-start | bytes 393224 | tf_op jit(solution)/shard_map/ppermute | solution.py:48
  272.3 5.4 %collective-permute-start.4 = (bf16[32,2,1024]{2,1,0:T(2,128)(2,1)S(1)}, bf16[32,2,1024]{2,1,0:T(2,128)(2,1)S(1)}, u32[]{:S(2)}, u32[]{:S(2)}) collective-permute-start(bf16[32,2,1024]{2,1,0:T(2,128)(2,1)S(1)} %collective-permute-done.3), channel_id=1, source_target_pairs={{0,16},{16,0},{1,17},{17,1},{2,18},{18,2},{3,19},{19,3},{4,20},{20... | collective-permute-start | bytes 393224 | tf_op jit(solution)/shard_map/ppermute | solution.py:48
  277.7 8.0 %collective-permute-start.5 = (bf16[32,2,1024]{2,1,0:T(2,128)(2,1)S(1)}, bf16[32,2,1024]{2,1,0:T(2,128)(2,1)S(1)}, u32[]{:S(2)}, u32[]{:S(2)}) collective-permute-start(bf16[32,2,1024]{2,1,0:T(2,128)(2,1)S(1)} %collective-permute-done.4), channel_id=1, source_target_pairs={{0,32},{32,0},{1,33},{33,1},{2,34},{34,2},{3,35},{35,3},{4,36},{36... | collective-permute-start | bytes 393224 | tf_op jit(solution)/shard_map/ppermute | solution.py:48
  285.6 11.8 %collective-permute-start.6 = (bf16[32,2,1024]{2,1,0:T(2,128)(2,1)S(1)}, bf16[32,2,1024]{2,1,0:T(2,128)(2,1)S(1)}, u32[]{:S(2)}, u32[]{:S(2)}) collective-permute-start(bf16[32,2,1024]{2,1,0:T(2,128)(2,1)S(1)} %collective-permute-done.5), channel_id=1, source_target_pairs={{0,64},{64,0},{1,65},{65,1},{2,66},{66,2},{3,67},{67,3},{4,68},{68... | collective-permute-start | bytes 393224 | tf_op jit(solution)/shard_map/ppermute | solution.py:48
where the time goes:
time: 303 us; the launch traced here: 299 us
  blocking collectives  75.8 us (25%)
  other arithmetic  56.5 us (19%)
  starting transfers between devices  49.9 us (16%)
  waiting for transfers between devices  49.7 us (16%)
  local copies, waits for them, and re-layouts  44.8 us (15%)
  matrix products  17.8 us (6%)
  between operations  3.74 us (1%)
    psum x3, blocking collectives, by_axis(): return functools.reduce(lax.psum, axes, array)  75.8 us
    ppermute x7, waiting for transfers between devices, from_partner(): return lax.ppermute(block, axis, route)  42.3 us
    all_to_all x1, starting transfers between devices, one_exchange(): tiles = lax.all_to_all(tiles, axis, split_axis=0, concat_axis=0, tiled=True)  30.3 us
    gather x1, local copies, waits for them, and re-layouts, local(): jnp.take(packed_rows, row_table, axis=0)  29.2 us
    convert_element_type x7, other arithmetic, add_block(): cosines.astype(jnp.bfloat16)  16.5 us
    mul x7, other arithmetic, add_block(): coarse_cos * fine_cos - coarse_sin * fine_sin  12.9 us
    dot_general x7, matrix products, add_block(): lax.dot_general(tables, masked, (((1,), (1,)), ((), ())), preferred_eleme...  12.1 us
    all_to_all x1, starting transfers between devices, local(): lax.all_to_all(outgoing, BAND_SUB, split_axis=0, concat_axis=0, tiled=True)  10.2 us
  transfers between devices with their start and end apart: 9, of which 8 were waited for; matrix products, arithmetic and copies ran while one was open for 1% of the time, Pallas kernels for 0%

commit v1 on v0

v1 whole, which is shorter than its diff:
```python
import functools

import jax
import jax.numpy as jnp
from jax import lax
from jax.experimental import pallas as pl
from jax.experimental.pallas import tpu as pltpu
from jax.sharding import Mesh
from jax.sharding import PartitionSpec as P

BAND_SUB = ("band_0", "band_1", "sub")
GROUPS_BAND_SUB = ("groups", "band_0", "band_1", "sub")

FINE = 256
GROUP = 8
VMEM_SPEC = pl.BlockSpec(memory_space=pltpu.VMEM)
SMEM_SPEC = pl.BlockSpec(memory_space=pltpu.SMEM)


def mod_units(units, modulus, inverse):
    quotient = jnp.floor(units.astype(jnp.float32) * inverse).astype(jnp.int32)
    rest = units - quotient * modulus
    rest = jnp.where(rest < 0, rest + modulus, rest)
    return jnp.where(rest >= modulus, rest - modulus, rest)


def turn(units, modulus, inverse, scale):
    angle = scale * mod_units(units, modulus, inverse).astype(jnp.float32)
    return jnp.cos(angle), jnp.sin(angle)


def combine(first, second):
    (a_cos, a_sin), (b_cos, b_sin) = first, second
    return a_cos * b_cos - a_sin * b_sin, a_sin * b_cos + a_cos * b_sin


def fourier_kernel(
    count_ref, offset_ref, orders_ref, mask_ref, maps_ref, coef_ref, sums_ref, table_ref, outer_ref, rows_ref
):
    pixel_slots = maps_ref.shape[1]
    rows = maps_ref.shape[0]
    maps_count = rows // 2
    slots = orders_ref.shape[1]
    count = count_ref[0]
    offset = offset_ref[0]
    count_float = count.astype(jnp.float32)
    modulus = 2 * count
    inverse = 1.0 / modulus.astype(jnp.float32)
    scale = jnp.pi / count_float
    orders = orders_ref[...]
    twice = 2 * orders
    coarse = pixel_slots // FINE
    near = 16
    step = lax.broadcasted_iota(jnp.int32, (near, slots), 0)
    low = turn(twice * step, modulus, inverse, scale)
    high = turn(twice * (near * step), modulus, inverse, scale)
    for index in range(FINE // near):
        here = tuple(part[index : index + 1] for part in high)
        cosine, sine = combine(here, low)
        table_ref[near * index : near * (index + 1), :slots] = cosine.astype(jnp.bfloat16)
        table_ref[near * index : near * (index + 1), slots:] = sine.astype(jnp.bfloat16)
    step = lax.broadcasted_iota(jnp.int32, (8, slots), 0)
    low = turn(twice * (FINE * step) + orders * offset, modulus, inverse, scale)
    high = turn(twice * (8 * FINE * step), modulus, inverse, scale)
    for index in range(coarse // 8):
        here = tuple(part[index : index + 1] for part in high)
        cosine, sine = combine(here, low)
        outer_ref[8 * index : 8 * (index + 1), :slots] = cosine
        outer_ref[8 * index : 8 * (index + 1), slots:] = sine
    pixels = lax.broadcasted_iota(jnp.int32, (1, pixel_slots), 1)
    mask = jnp.where(pixels < count, mask_ref[...], 0.0)
    square = jnp.sum(mask * mask)
    table = table_ref[...]
    real_sum = jnp.zeros((rows, slots), jnp.float32)
    imag_sum = jnp.zeros((rows, slots), jnp.float32)
    for group in range(coarse // GROUP):
        buffer = rows_ref.at[group % 2]
        for member in range(GROUP):
            first = (group * GROUP + member) * FINE
            block = maps_ref[:, first : first + FINE].astype(jnp.float32) * mask[:, first : first + FINE]
            buffer[member * rows : (member + 1) * rows, :] = block.astype(jnp.bfloat16)
        inner = jnp.dot(buffer[...], table, preferred_element_type=jnp.float32)
        for member in range(GROUP):
            index = group * GROUP + member
            cosine = outer_ref[index : index + 1, :slots]
            sine = outer_ref[index : index + 1, slots:]
            inner_cos = inner[member * rows : (member + 1) * rows, :slots]
            inner_sin = inner[member * rows : (member + 1) * rows, slots:]
            real_sum = real_sum + (cosine * inner_cos - sine * inner_sin)
            imag_sum = imag_sum + (sine * inner_cos + cosine * inner_sin)
    inverse_root = 1.0 / jnp.sqrt(count_float)
    live = twice < count
    real_part = jnp.where(live, real_sum * inverse_root, 0.0)
    imag_part = jnp.where(live, -imag_sum * inverse_root, 0.0)
    joined = jnp.concatenate(
        [real_part[:maps_count], imag_part[:maps_count], real_part[maps_count:], imag_part[maps_count:]], axis=0
    )
    half = slots // 2
    coef_ref[0] = jnp.transpose(joined[:, :half]).astype(jnp.bfloat16)
    coef_ref[1] = jnp.transpose(joined[:, half:]).astype(jnp.bfloat16)
    lane = lax.broadcasted_iota(jnp.int32, sums_ref.shape, 1)
    value = jnp.where(lane < 3, square, count_float)
    top = value.astype(jnp.bfloat16).astype(jnp.float32)
    middle = (value - top).astype(jnp.bfloat16).astype(jnp.float32)
    bottom = ((value - top) - middle).astype(jnp.bfloat16).astype(jnp.float32)
    kind = lane % 3
    pieces = jnp.where(kind == 0, top, jnp.where(kind == 1, middle, bottom))
    sums_ref[...] = jnp.where(lane < 6, pieces, 0.0).astype(jnp.bfloat16)


def fourier(maps, mask, count, offset, orders):
    rows, pixel_slots = maps.shape
    slots = orders.shape[1]
    return pl.pallas_call(
        fourier_kernel,
        out_shape=(
            jax.ShapeDtypeStruct((2, slots // 2, 2 * rows), jnp.bfloat16),
            jax.ShapeDtypeStruct((1, 2 * rows), jnp.bfloat16),
        ),
        in_specs=[SMEM_SPEC, SMEM_SPEC, VMEM_SPEC, VMEM_SPEC, VMEM_SPEC],
        out_specs=(VMEM_SPEC, VMEM_SPEC),
        scratch_shapes=[
            pltpu.VMEM((FINE, 2 * slots), jnp.bfloat16),
            pltpu.VMEM((pixel_slots // FINE, 2 * slots), jnp.float32),
            pltpu.VMEM((2, GROUP * rows, FINE), jnp.bfloat16),
        ],
        name="fourier",
    )(count, offset, orders, mask, maps)


def reversed_rows(block):
    rows = block.shape[0]
    index = 7 - lax.broadcasted_iota(jnp.int32, (8, block.shape[1]), 0)
    tiles = [
        jnp.take_along_axis(block[8 * t : 8 * (t + 1)], index, axis=0) for t in range(rows // 8)
    ]
    return jnp.concatenate(tiles[::-1], axis=0)


def alm_kernel(order_ref, coef_ref, legendre_ref, alm_ref, send_ref, operand_ref, held_ref):
    tile = pl.program_id(0)
    tiles = pl.num_programs(0)
    height = legendre_ref.shape[0]
    columns = coef_ref.shape[2]
    quarter = columns // 4
    degrees = held_ref.shape[0] - 64
    order = order_ref[0]
    split = degrees - order

    @pl.when(tile == 0)
    def _():
        row = lax.broadcasted_iota(jnp.int32, (columns, columns), 0)
        column = lax.broadcasted_iota(jnp.int32, (columns, columns), 1)
        part = column // quarter
        hit = (row // quarter == 3 - part) & (row % quarter == column % quarter)
        sign = jnp.where((part == 1) | (part == 2), -1.0, 1.0)
        swap = jnp.where(hit, sign, 0.0).astype(jnp.bfloat16)
        for slot in range(2):
            block = coef_ref[slot]
            lower = jnp.dot(block, swap, preferred_element_type=jnp.float32)
            operand_ref[slot, : block.shape[0]] = -block
            operand_ref[slot, block.shape[0] :] = (-lower).astype(jnp.bfloat16)

    first_row = tile * height
    rows = legendre_ref[...]
    slot = (first_row >= split).astype(jnp.int32)
    product = jnp.dot(rows, operand_ref[slot], preferred_element_type=jnp.float32)
    alm_ref[...] = product
    held_ref[pl.ds(32 + pl.multiple_of(first_row, height), height)] = product

    @pl.when((first_row < split) & (split < first_row + height))
    def _():
        other = jnp.dot(rows, operand_ref[1], preferred_element_type=jnp.float32)
        row_index = first_row + lax.broadcasted_iota(jnp.int32, (height, 1), 0)
        fixed = jnp.where(row_index >= split, other, product)
        alm_ref[...] = fixed
        held_ref[pl.ds(32 + pl.multiple_of(first_row, height), height)] = fixed

    @pl.when(tile == tiles - 1)
    def _():
        devices = send_ref.shape[0] // 64
        step = lax.broadcasted_iota(jnp.int32, (32, 1), 0)

        def one(device, carry):
            upper = device >= devices // 2
            block = jnp.where(upper, devices - 1 - device, device)
            low = 64 * block + 32 * upper.astype(jnp.int32)
            kept = held_ref[pl.ds(32 + jnp.maximum(low - order, -32), 32)]
            moved = reversed_rows(held_ref[pl.ds(pl.multiple_of(degrees - low, 32), 32)])
            mirror = reversed_rows(held_ref[pl.ds(degrees - low - order, 32)])
            start = pl.multiple_of(device * 64, 64)
            send_ref[pl.ds(start, 32)] = jnp.where(step >= order - low, kept, moved).astype(jnp.bfloat16)
            send_ref[pl.ds(start + 32, 32)] = mirror.astype(jnp.bfloat16)
            return carry

        lax.fori_loop(0, devices, one, 0, unroll=2)


def alm_and_send(order, coef, legendre, height=512):
    degrees, inner = legendre.shape
    columns = coef.shape[2]
    return pl.pallas_call(
        alm_kernel,
        grid=(degrees // height,),
        out_shape=(
            jax.ShapeDtypeStruct((degrees, columns), jnp.float32),
            jax.ShapeDtypeStruct((degrees, columns), jnp.bfloat16),
        ),
        in_specs=[
            SMEM_SPEC,
            VMEM_SPEC,
            pl.BlockSpec((height, inner), lambda t: (t, 0)),
        ],
        out_specs=(pl.BlockSpec((height, columns), lambda t: (t, 0)), VMEM_SPEC),
        scratch_shapes=[
            pltpu.VMEM((2, inner, columns), jnp.bfloat16),
            pltpu.VMEM((degrees + 64, columns), jnp.float32),
        ],
        compiler_params=pltpu.CompilerParams(dimension_semantics=("arbitrary",)),
        name="alm_and_send",
    )(order, coef, legendre)


def outer_totals(rows, maps_count):
    split_parts = rows.reshape(rows.shape[0], rows.shape[1], 2, 2, maps_count)
    return jnp.einsum(
        "slerm,slern->lemn", split_parts, split_parts, preferred_element_type=jnp.float32
    )


def scaled_spectra(totals, degrees, orders, weight, maps_count):
    counts = jnp.maximum(
        jnp.sum((orders[None, :] <= degrees[:, None]).astype(jnp.int32), axis=1), 1
    ).astype(jnp.float32)
    return (2.0 * totals / (weight * counts)[:, None, None, None]).reshape(
        degrees.shape[0], 2, maps_count * maps_count
    )


def local(sky_maps, sky_mask, pixel_counts, phi_offsets, low_orders, legendre):
    devices = lax.axis_size(BAND_SUB)
    device_index = lax.axis_index(BAND_SUB)
    degree_count = legendre.shape[1]
    maps_count = sky_maps.shape[2]
    columns = 4 * maps_count
    orders = jnp.concatenate([low_orders, degree_count - low_orders])
    coef, sums = fourier(
        sky_maps.reshape(2 * maps_count, sky_maps.shape[3]), sky_mask, pixel_counts, phi_offsets, orders[None]
    )
    outgoing = jnp.concatenate(
        [jnp.swapaxes(coef, 0, 1), jnp.broadcast_to(sums[:, None], (devices, 2, columns))], axis=1
    )
    received = lax.all_to_all(outgoing, BAND_SUB, split_axis=0, concat_axis=0, tiled=True)
    blocks = jnp.swapaxes(received[:, :2], 0, 1)
    pieces = received[:, 2, :6].astype(jnp.float32)
    totals = jnp.sum(pieces.reshape(devices, 2, 3).sum(axis=2), axis=0)
    weight = totals[0] / totals[1]
    order = lax.dynamic_slice_in_dim(low_orders, device_index, 1, 0)
    alm, send = alm_and_send(order, blocks, legendre[0])
    range_rows = degree_count // devices
    half_rows = range_rows // 2
    incoming = lax.all_to_all(
        send.reshape(devices, range_rows, columns), BAND_SUB, split_axis=0, concat_axis=0, tiled=True
    )
    upper_device = device_index >= devices // 2
    pair_block = jnp.minimum(device_index, devices - 1 - device_index)
    own_low = (
        pair_block * range_rows
        + upper_device.astype(jnp.int32) * half_rows
        + jnp.arange(half_rows, dtype=jnp.int32)
    )
    own_mirror = degree_count - 1 - own_low
    kept_mask = own_low[None, :] >= low_orders[:, None]
    low_rows = incoming[:, :half_rows]
    mirror_rows = incoming[:, half_rows:]
    low_kept = jnp.where(kept_mask[:, :, None], low_rows, jnp.zeros_like(low_rows))
    low_moved = jnp.where(kept_mask[:, :, None], jnp.zeros_like(low_rows), low_rows)
    low_totals = outer_totals(low_kept, maps_count)
    mirror_totals = outer_totals(mirror_rows, maps_count) + outer_totals(low_moved, maps_count)
    low_spectra = scaled_spectra(low_totals, own_low, orders, weight, maps_count)
    mirror_spectra = jnp.flip(
        scaled_spectra(mirror_totals, own_mirror, orders, weight, maps_count), axis=0
    )
    swapped = jnp.where(upper_device, low_spectra, mirror_spectra)
    route = [(device, devices - 1 - device) for device in range(devices)]
    swapped = lax.ppermute(swapped.astype(jnp.bfloat16), BAND_SUB, route).astype(jnp.float32)
    spectra = jnp.where(
        upper_device,
        jnp.concatenate([mirror_spectra, swapped], axis=0),
        jnp.concatenate([low_spectra, swapped], axis=0),
    )
    return (alm[None], spectra)


def solution(mesh):
    torus = Mesh(
        mesh.devices.reshape(mesh.shape["groups"], 8, 8, mesh.shape["sub"]),
        ("groups", "band_0", "band_1", "sub"),
    )
    in_specs = (
        P(GROUPS_BAND_SUB, None, None, None),
        P(GROUPS_BAND_SUB, None),
        P(GROUPS_BAND_SUB),
        P(GROUPS_BAND_SUB),
        P("groups"),
        P(GROUPS_BAND_SUB, None, None),
    )
    out_specs = (P(GROUPS_BAND_SUB, None, None), P(GROUPS_BAND_SUB, None, None))
    return jax.shard_map(local, mesh=torus, in_specs=in_specs, out_specs=out_specs, check_vma=False)
```

time: 303 us -> 154 us (0.51)
  the two profiles are of different devices: /device:TPU:518 before, /device:TPU:514 now
where the time goes in v1:
time: 154 us; the launch traced here: 153 us
  waiting for transfers between devices  73.7 us (48%)
  starting transfers between devices  34.8 us (23%)
  Pallas kernels  19.3 us (13%)
  local copies, waits for them, and re-layouts  10.4 us (7%)
  other arithmetic  6.84 us (4%)
  matrix products  4.9 us (3%)
  between operations  3.42 us (2%)
    all_to_all x1, waiting for transfers between devices, local(): lax.all_to_all(send.reshape(devices, range_rows, columns), BAND_SUB, spli...  50.7 us
    all_to_all x1, starting transfers between devices, local(): lax.all_to_all(outgoing, BAND_SUB, split_axis=0, concat_axis=0, tiled=True)  26.4 us
    pallas_call x1, Pallas kernels, alm_and_send(): pl.pallas_call(alm_kernel, grid=(degrees // height,), out_shape=(jax.Shap...  14.7 us
    ppermute x1, waiting for transfers between devices, local(): lax.ppermute(swapped.astype(jnp.bfloat16), BAND_SUB, route)  11.8 us
    all_to_all x1, waiting for transfers between devices, local(): lax.all_to_all(outgoing, BAND_SUB, split_axis=0, concat_axis=0, tiled=True)  11.2 us
    all_to_all x1, starting transfers between devices, local(): lax.all_to_all(send.reshape(devices, range_rows, columns), BAND_SUB, spli...  8.24 us
    dot_general x3, matrix products, outer_totals(): jnp.einsum('slerm,slern->lemn', split_parts, split_parts, preferred_eleme...  4.9 us
    pallas_call x1, Pallas kernels, fourier(): pl.pallas_call(fourier_kernel, out_shape=(jax.ShapeDtypeStruct((2, slots...  4.63 us
  transfers between devices with their start and end apart: 3, of which 3 were waited for; matrix products, arithmetic and copies ran while one was open for 1% of the time, Pallas kernels for 0%

profile of v1, /device:TPU:514, one launch (start us, length us, event | category | flops | bytes accessed | tf_op | source)
XLA Modules:
  0.0 153.5 jit_solution(10905547081603128676)
XLA Ops:
  0.6 0.0 copy-start.3
  1.9 0.7 broadcast_subtract_fusion.1
  2.6 1.2 pad_add_fusion
  3.8 4.6 %fourier.1 = (bf16[2,128,128]{2,1,0:T(8,128)(2,1)}, bf16[1,128]{1,0:T(2,128)(2,1)}) custom-call(s32[1]{0:T(128)S(6)} %copy.27.count_ref, s32[1]{0:T(128)S(6)} %copy.28.offset_ref, s32[1,256]{1,0:T(1,128)} %bitcast.51, f32[1,16384]{1,0:T(1,128)} %mask_ref.1, bf16[64,16384]{1,0:T(8,128)(2,1)} %bitcast.45), custom_call_target="tpu_custom_call" | custom-call | tf_op jit(solution)/shard_map/fourier/pallas_call | solution.py:114
  8.5 0.7 broadcast_in_dim.21
  9.1 0.9 pad_maximum_fusion.2
  10.0 0.8 copy.16
  10.7 26.4 %all-to-all-start = ((bf16[128,4,128]{2,1,0:T(4,128)(2,1)}), bf16[128,4,128]{2,1,0:T(4,128)(2,1)S(1)}, u32[]{:S(2)}, u32[]{:S(2)}) async-start(bf16[128,4,128]{2,1,0:T(4,128)(2,1)} %copy.16), calls=%async_computation | async-start | bytes 262144 | tf_op jit(solution)/shard_map/all_to_all | solution.py:253
  37.2 0.0 copy-done.3
  37.2 0.6 dynamic_slice.3.order_ref
  37.8 11.2 %all-to-all-done = bf16[128,4,128]{2,1,0:T(4,128)(2,1)S(1)} async-done(((bf16[128,4,128]{2,1,0:T(4,128)(2,1)}), bf16[128,4,128]{2,1,0:T(4,128)(2,1)S(1)}, u32[]{:S(2)}, u32[]{:S(2)}) %all-to-all-start) | async-done | bytes 131104 | tf_op jit(solution)/shard_map/all_to_all | solution.py:253
  49.0 0.6 copy.26
  49.7 14.7 %alm_and_send.1 = (f32[8192,128]{1,0:T(8,128)}, bf16[8192,128]{1,0:T(8,128)(2,1)}) custom-call(s32[1]{0:T(128)} %dynamic_slice.3.order_ref, bf16[2,128,128]{2,1,0:T(8,128)(2,1)} %bitcast.49, bf16[8192,256]{1,0:T(8,128)(2,1)} %bitcast.44), custom_call_target="tpu_custom_call" | custom-call | tf_op jit(solution)/shard_map/alm_and_send/pallas_call | solution.py:202
  64.4 0.0 copy-start.2
  64.4 8.2 %all-to-all-start.1 = ((bf16[128,64,128]{2,1,0:T(8,128)(2,1)}), bf16[128,64,128]{2,1,0:T(8,128)(2,1)S(1)}, u32[]{:S(2)}, u32[]{:S(2)}) async-start(bf16[128,64,128]{2,1,0:T(8,128)(2,1)} %bitcast.46), calls=%async_computation.1 | async-start | bytes 4194304 | tf_op jit(solution)/shard_map/all_to_all | solution.py:262
  72.7 0.0 copy-done.2
  72.7 0.2 convert_reduce_fusion.1
  72.9 0.1 broadcast_compare_fusion
  72.9 0.2 fusion.6
  73.1 0.1 reduce_sum.39
  73.2 0.1 reduce_sum.40
  73.3 0.6 fusion.7
  75.2 50.7 %all-to-all-done.1 = bf16[128,64,128]{2,1,0:T(8,128)(2,1)S(1)} async-done(((bf16[128,64,128]{2,1,0:T(8,128)(2,1)}), bf16[128,64,128]{2,1,0:T(8,128)(2,1)S(1)}, u32[]{:S(2)}, u32[]{:S(2)}) %all-to-all-start.1) | async-done | bytes 2097184 | tf_op jit(solution)/shard_map/all_to_all | solution.py:262
  125.9 2.2 %broadcast_select_fusion.1 = (bf16[128,32,128]{2,1,0:T(8,128)(2,1)}, bf16[128,32,128]{2,1,0:T(8,128)(2,1)}, bf16[128,32,128]{2,1,0:T(8,128)(2,1)S(1)}) fusion(pred[128,32]{1,0:T(8,128)(4,1)S(1)} %broadcast_compare_fusion, bf16[128,64,128]{2,1,0:T(8,128)(2,1)S(1)} %all-to-all-done.1), kind=kLoop, calls=%fused_computation.9 | loop fusion | flops 1048576 | bytes 5246976 | tf_op jit(solution)/shard_map/jit(_where)/select_n | solution.py:277
  128.2 1.9 %copy.19 = bf16[128,32,128]{0,2,1:T(8,128)(2,1)S(1)} copy(bf16[128,32,128]{2,1,0:T(8,128)(2,1)} %get-tuple-element.12) | data formatting | bytes 2097152 | tf_op jit(solution)/shard_map/jit(_where)/select_n | solution.py:277
  130.1 0.0 copy-start
  130.1 1.4 convolution_bitcast_fusion.1
  131.5 0.0 copy-done
  131.5 1.0 copy.20
  132.5 1.4 fusion.1
  133.9 0.0 copy-start.1
  133.9 1.9 %reshape.86 = f32[32,2,1024]{2,1,0:T(2,128)S(1)} reshape(f32[32,2,32,32]{3,2,1,0:T(8,128)} %fusion.1) | data formatting | bytes 524288 | tf_op jit(solution)/shard_map/reshape | solution.py:235
  135.8 1.7 %copy.18 = bf16[128,32,128]{0,2,1:T(8,128)(2,1)} copy(bf16[128,32,128]{2,1,0:T(8,128)(2,1)S(1)} %get-tuple-element.14) | data formatting | bytes 2097152 | tf_op jit(solution)/shard_map/slice | solution.py:275
  137.4 0.0 copy-done.1
  137.5 2.1 %fusion.4 = f32[32,2,32,32]{3,2,1,0:T(8,128)S(1)} fusion(f32[32,2,32,32]{3,2,1,0:T(8,128)S(1)} %copy-done.1, bf16[128,32,2,2,32]{0,4,3,2,1:T(8,128)(2,1)} %bitcast.47, f32[32]{0:T(128)S(1)} %get-tuple-element.18), kind=kOutput, calls=%fused_computation.7 | convolution fusion | flops 33751040 | bytes 1572992 | tf_op jit(solution)/shard_map/slerm,slern->lemn/dot_general | solution.py:226
  139.5 0.6 reshape.84
  140.1 0.1 select_convert_fusion
  140.3 0.1 collective-permute-start
  140.4 11.8 %collective-permute-done = bf16[32,2,1024]{2,1,0:T(2,128)(2,1)S(1)} collective-permute-done((bf16[32,2,1024]{2,1,0:T(2,128)(2,1)S(1)}, bf16[32,2,1024]{2,1,0:T(2,128)(2,1)S(1)}, u32[]{:S(2)}, u32[]{:S(2)}) %collective-permute-start) | collective-permute-done | bytes 131104 | tf_op jit(solution)/shard_map/ppermute | solution.py:286
  152.3 0.1 convert_element_type.38
  152.4 1.1 fusion.5
  (5 shorter events, 0.1 us)
Async XLA Ops:
  0.6 36.6 %copy-start.3 = (s32[128]{0:T(128)S(1)}, s32[128]{0:T(128)}, u32[]{:S(2)}) copy-start(s32[128]{0:T(128)} %param.10) | copy-start | bytes 1540
  10.7 38.2 %all-to-all-start = ((bf16[128,4,128]{2,1,0:T(4,128)(2,1)}), bf16[128,4,128]{2,1,0:T(4,128)(2,1)S(1)}, u32[]{:S(2)}, u32[]{:S(2)}) async-start(bf16[128,4,128]{2,1,0:T(4,128)(2,1)} %copy.16), calls=%async_computation | async-start | bytes 262144 | tf_op jit(solution)/shard_map/all_to_all | solution.py:253
  64.4 8.3 %copy-start.2 = (s32[256]{0:T(256)S(1)}, s32[256]{0:T(256)}, u32[]{:S(2)}) copy-start(s32[256]{0:T(256)} %pad_add_fusion) | copy-start | bytes 3076
  64.4 61.6 %all-to-all-start.1 = ((bf16[128,64,128]{2,1,0:T(8,128)(2,1)}), bf16[128,64,128]{2,1,0:T(8,128)(2,1)S(1)}, u32[]{:S(2)}, u32[]{:S(2)}) async-start(bf16[128,64,128]{2,1,0:T(8,128)(2,1)} %bitcast.46), calls=%async_computation.1 | async-start | bytes 4194304 | tf_op jit(solution)/shard_map/all_to_all | solution.py:262
  130.1 1.4 copy-start
  133.9 3.6 %copy-start.1 = (f32[32,2,32,32]{3,2,1,0:T(8,128)S(1)}, f32[32,2,32,32]{3,2,1,0:T(8,128)}, u32[]{:S(2)}) copy-start(f32[32,2,32,32]{3,2,1,0:T(8,128)} %convolution_bitcast_fusion.1) | copy-start | bytes 786436
  140.3 12.0 %collective-permute-start = (bf16[32,2,1024]{2,1,0:T(2,128)(2,1)S(1)}, bf16[32,2,1024]{2,1,0:T(2,128)(2,1)S(1)}, u32[]{:S(2)}, u32[]{:S(2)}) collective-permute-start(bf16[32,2,1024]{2,1,0:T(2,128)(2,1)S(1)} %select_convert_fusion), channel_id=1, source_target_pairs={{0,127},{1,126},{2,125},{3,124},{4,123},{5,122},{6,121},{7,120},{8... | collective-permute-start | bytes 393224 | tf_op jit(solution)/shard_map/ppermute | solution.py:286

commit v2 on v1

v2 whole, which is shorter than its diff:
```python
import functools

import jax
import jax.numpy as jnp
from jax import lax
from jax.experimental import pallas as pl
from jax.experimental.pallas import tpu as pltpu
from jax.sharding import Mesh
from jax.sharding import PartitionSpec as P

BAND_SUB = ("band_0", "band_1", "sub")
GROUPS_BAND_SUB = ("groups", "band_0", "band_1", "sub")
CHUNKS = 1

FINE = 256
GROUP = 8
PITCH = 132
VMEM_SPEC = pl.BlockSpec(memory_space=pltpu.VMEM)
SMEM_SPEC = pl.BlockSpec(memory_space=pltpu.SMEM)
ANY_SPEC = pl.BlockSpec(memory_space=pl.ANY)


def mod_units(units, modulus, inverse):
    quotient = jnp.floor(units.astype(jnp.float32) * inverse).astype(jnp.int32)
    rest = units - quotient * modulus
    rest = jnp.where(rest < 0, rest + modulus, rest)
    return jnp.where(rest >= modulus, rest - modulus, rest)


def turn(units, modulus, inverse, scale):
    angle = scale * mod_units(units, modulus, inverse).astype(jnp.float32)
    return jnp.cos(angle), jnp.sin(angle)


def combine(first, second):
    (a_cos, a_sin), (b_cos, b_sin) = first, second
    return a_cos * b_cos - a_sin * b_sin, a_sin * b_cos + a_cos * b_sin


def fourier_kernel(
    degrees, count_ref, offset_ref, order_ref, mask_ref, maps_ref, out_ref, table_ref, outer_ref, rows_ref, join_ref
):
    pixel_slots = maps_ref.shape[1]
    rows = maps_ref.shape[0]
    maps_count = rows // 2
    pairs = order_ref.shape[1]
    slots = 2 * pairs
    count = count_ref[0]
    offset = offset_ref[0]
    count_float = count.astype(jnp.float32)
    modulus = 2 * count
    inverse = 1.0 / modulus.astype(jnp.float32)
    scale = jnp.pi / count_float
    low_orders = order_ref[...]
    orders = jnp.concatenate([low_orders, degrees - low_orders], axis=1)
    twice = 2 * orders
    coarse = pixel_slots // FINE
    near = 16
    step = lax.broadcasted_iota(jnp.int32, (near, slots), 0)
    low = turn(twice * step, modulus, inverse, scale)
    high = turn(twice * (near * step), modulus, inverse, scale)
    for index in range(FINE // near):
        here = tuple(part[index : index + 1] for part in high)
        cosine, sine = combine(here, low)
        table_ref[near * index : near * (index + 1), :slots] = cosine.astype(jnp.bfloat16)
        table_ref[near * index : near * (index + 1), slots:] = sine.astype(jnp.bfloat16)
    step = lax.broadcasted_iota(jnp.int32, (8, slots), 0)
    low = turn(twice * (FINE * step) + orders * offset, modulus, inverse, scale)
    high = turn(twice * (8 * FINE * step), modulus, inverse, scale)
    for index in range(coarse // 8):
        here = tuple(part[index : index + 1] for part in high)
        cosine, sine = combine(here, low)
        outer_ref[8 * index : 8 * (index + 1), :slots] = cosine
        outer_ref[8 * index : 8 * (index + 1), slots:] = sine
    pixels = lax.broadcasted_iota(jnp.int32, (1, pixel_slots), 1)
    mask = jnp.where(pixels < count, mask_ref[...], 0.0)
    square = jnp.sum(mask * mask)
    table = table_ref[...]
    real_sum = jnp.zeros((rows, slots), jnp.float32)
    imag_sum = jnp.zeros((rows, slots), jnp.float32)
    for group in range(coarse // GROUP):
        buffer = rows_ref.at[group % 2]
        for member in range(GROUP):
            first = (group * GROUP + member) * FINE
            block = maps_ref[:, first : first + FINE].astype(jnp.float32) * mask[:, first : first + FINE]
            buffer[member * rows : (member + 1) * rows, :] = block.astype(jnp.bfloat16)
        inner = jnp.dot(buffer[...], table, preferred_element_type=jnp.float32)
        for member in range(GROUP):
            index = group * GROUP + member
            cosine = outer_ref[index : index + 1, :slots]
            sine = outer_ref[index : index + 1, slots:]
            inner_cos = inner[member * rows : (member + 1) * rows, :slots]
            inner_sin = inner[member * rows : (member + 1) * rows, slots:]
            real_sum = real_sum + (cosine * inner_cos - sine * inner_sin)
            imag_sum = imag_sum + (sine * inner_cos + cosine * inner_sin)
    inverse_root = 1.0 / jnp.sqrt(count_float)
    live = twice < count
    real_part = jnp.where(live, real_sum * inverse_root, 0.0)
    imag_part = jnp.where(live, -imag_sum * inverse_root, 0.0)
    joined = jnp.concatenate(
        [real_part[:maps_count], imag_part[:maps_count], real_part[maps_count:], imag_part[maps_count:]], axis=0
    )
    join_ref[pl.ds(0, pairs, stride=4)] = jnp.transpose(joined[:, :pairs])
    join_ref[pl.ds(1, pairs, stride=4)] = jnp.transpose(joined[:, pairs:])
    lane = lax.broadcasted_iota(jnp.int32, (1, 2 * rows), 1)
    value = jnp.where(lane < 3, square, count_float)
    top = value.astype(jnp.bfloat16).astype(jnp.float32)
    middle = (value - top).astype(jnp.bfloat16).astype(jnp.float32)
    bottom = ((value - top) - middle).astype(jnp.bfloat16).astype(jnp.float32)
    kind = lane % 3
    pieces = jnp.where(kind == 0, top, jnp.where(kind == 1, middle, bottom))
    pieces = jnp.broadcast_to(jnp.where(lane < 6, pieces, 0.0), (pairs, 2 * rows))
    join_ref[pl.ds(2, pairs, stride=4)] = pieces
    join_ref[pl.ds(3, pairs, stride=4)] = pieces
    out_ref[...] = join_ref[...].astype(jnp.bfloat16)


def fourier(maps, mask, count, offset, low_orders, degrees):
    rows, pixel_slots = maps.shape
    pairs = low_orders.shape[1]
    slots = 2 * pairs
    return pl.pallas_call(
        functools.partial(fourier_kernel, degrees),
        out_shape=jax.ShapeDtypeStruct((4 * pairs, 2 * rows), jnp.bfloat16),
        in_specs=[SMEM_SPEC, SMEM_SPEC, VMEM_SPEC, VMEM_SPEC, VMEM_SPEC],
        out_specs=VMEM_SPEC,
        scratch_shapes=[
            pltpu.VMEM((FINE, 2 * slots), jnp.bfloat16),
            pltpu.VMEM((pixel_slots // FINE, 2 * slots), jnp.float32),
            pltpu.VMEM((2, GROUP * rows, FINE), jnp.bfloat16),
            pltpu.VMEM((4 * pairs, 2 * rows), jnp.float32),
        ],
        name="fourier",
    )(count, offset, low_orders, mask, maps)


def alm_kernel(
    chunks, height, order_ref, given_ref, legendre_ref, alm_ref, weight_ref, *rest
):
    send_refs = rest[:chunks]
    given32_ref, operand_ref, held_ref, sem = rest[chunks:]
    columns = given_ref.shape[1]
    cycles = given_ref.shape[0] // 4
    quarter = columns // 4
    degrees = legendre_ref.shape[0]
    order = order_ref[0]
    split = degrees - order
    given32_ref[...] = given_ref[...].astype(jnp.float32)
    row = lax.broadcasted_iota(jnp.int32, (columns, columns), 0)
    column = lax.broadcasted_iota(jnp.int32, (columns, columns), 1)
    part = column // quarter
    hit = (row // quarter == 3 - part) & (row % quarter == column % quarter)
    sign = jnp.where((part == 1) | (part == 2), -1.0, 1.0)
    swap = jnp.where(hit, sign, 0.0).astype(jnp.bfloat16)
    for slot in range(2):
        block = given32_ref[pl.ds(slot, cycles, stride=4)].astype(jnp.bfloat16)
        lower = jnp.dot(block, swap, preferred_element_type=jnp.float32)
        operand_ref[slot, :cycles] = -block
        operand_ref[slot, cycles:] = (-lower).astype(jnp.bfloat16)

    for tile in range(degrees // height):
        first_row = tile * height
        rows = legendre_ref[first_row : first_row + height]
        slot = (first_row >= split).astype(jnp.int32)
        held_ref[32 + first_row : 32 + first_row + height] = jnp.dot(
            rows, operand_ref[slot], preferred_element_type=jnp.float32
        )
    border = pl.multiple_of(split // height * height, height)
    other = jnp.dot(legendre_ref[pl.ds(border, height)], operand_ref[1], preferred_element_type=jnp.float32)
    row_index = border + lax.broadcasted_iota(jnp.int32, (height, 1), 0)
    place = pl.ds(32 + border, height)
    held_ref[place] = jnp.where(row_index >= split, other, held_ref[place])
    copy = pltpu.make_async_copy(held_ref.at[pl.ds(32, degrees)], alm_ref, sem)
    copy.start()

    pieces = given32_ref[pl.ds(2, cycles, stride=4)]
    lane = lax.broadcasted_iota(jnp.int32, pieces.shape, 1)
    square = jnp.sum(jnp.where(lane < 3, pieces, 0.0))
    pixels = jnp.sum(jnp.where(lane < 3, 0.0, pieces))
    weight_ref[...] = jnp.full(weight_ref.shape, square / pixels, jnp.float32)

    half = send_refs[0].shape[0] // cycles // 2
    step = lax.broadcasted_iota(jnp.int32, (half, 1), 0)

    def one(device, carry):
        upper = device >= cycles // 2
        block = jnp.where(upper, cycles - 1 - device, device)
        start = pl.multiple_of(device * 2 * half, 2 * half)
        for chunk in range(chunks):
            low = 2 * chunks * half * block + chunks * half * upper.astype(jnp.int32) + chunk * half
            kept = held_ref[pl.ds(32 + jnp.maximum(low - order, -half), half)]
            moved = held_ref[pl.ds(32 + degrees - jnp.minimum(low + half, order), half)]
            mirror = held_ref[pl.ds(32 + degrees - half - low - order, half)]
            mixed = jnp.where(step >= order - low, kept, moved)
            send_refs[chunk][pl.ds(start, half)] = mixed.astype(jnp.bfloat16)
            send_refs[chunk][pl.ds(start + half, half)] = mirror.astype(jnp.bfloat16)
        return carry

    lax.fori_loop(0, cycles, one, 0, unroll=4)
    copy.wait()


def alm_and_send(order, given, legendre, chunks, height=512):
    degrees, inner = legendre.shape
    columns = given.shape[1]
    send = jax.ShapeDtypeStruct((degrees // chunks, columns), jnp.bfloat16)
    return pl.pallas_call(
        functools.partial(alm_kernel, chunks, height),
        out_shape=(
            jax.ShapeDtypeStruct((degrees, columns), jnp.float32),
            jax.ShapeDtypeStruct((1, columns), jnp.float32),
        )
        + (send,) * chunks,
        in_specs=[SMEM_SPEC, VMEM_SPEC, VMEM_SPEC],
        out_specs=(ANY_SPEC, VMEM_SPEC) + (VMEM_SPEC,) * chunks,
        scratch_shapes=[
            pltpu.VMEM(given.shape, jnp.float32),
            pltpu.VMEM((2, inner, columns), jnp.bfloat16),
            pltpu.VMEM((degrees + 64, columns), jnp.float32),
            pltpu.SemaphoreType.DMA,
        ],
        name="alm_and_send",
    )(order, given, legendre)


def spectra_kernel(
    chunk, degrees, start_ref, order_ref, order_row_ref, weight_ref, rows_ref, low_ref, mirror_ref,
    kept_ref, moved_ref, mirrored_ref, gram_ref, factor_ref,
):
    pairs = order_row_ref.shape[1]
    half = rows_ref.shape[0] // pairs // 2
    first = start_ref[0] + chunk * half
    step = lax.broadcasted_iota(jnp.int32, (half, 1), 0)
    columns = rows_ref.shape[1]
    quarter = columns // 4
    moved_ref[0 : half * PITCH] = jnp.zeros((half * PITCH, columns), jnp.float32)

    def one(pair, carry):
        start = pl.multiple_of(pair * 2 * half, 2 * half)
        block = rows_ref[pl.ds(start, 2 * half)].astype(jnp.float32)
        order = order_ref[pair]
        early = jnp.clip(order - first, 0, half)
        kept_ref[pl.ds(pair, half, stride=PITCH)] = jnp.where(step >= early, block[:half], 0.0)
        moved_ref[pl.ds((half - early) * PITCH + pair, half, stride=PITCH)] = block[:half]
        mirrored_ref[pl.ds(pair, half, stride=PITCH)] = block[half:]
        return carry

    lax.fori_loop(0, pairs, one, 0, unroll=4)

    orders = order_row_ref[...]
    weight = weight_ref[...]
    low_degree = first + step
    mirror_degree = degrees - half - first + step
    for kind, degree in enumerate((low_degree, mirror_degree)):
        below = (orders <= degree).astype(jnp.float32) + (degrees - orders <= degree).astype(jnp.float32)
        counts = jnp.maximum(jnp.sum(below, axis=1, keepdims=True), 1.0)
        factor_ref[kind * half : (kind + 1) * half] = 2.0 / (weight * counts)

    def gram(rows):
        return lax.dot_general(rows, rows, (((0,), (0,)), ((), ())), preferred_element_type=jnp.float32)

    lane_group = lax.broadcasted_iota(jnp.int32, (8, columns), 1) // quarter

    def flat(total, slot, out_ref, index, factor):
        for part in range(2):
            base = 2 * part * quarter
            real = total[base : base + quarter]
            imag = total[base + quarter : base + 2 * quarter]
            gram_ref[2 * slot + part] = real + pltpu.roll(imag, columns - quarter, 1)
            row = None
            for member in range(4):
                piece = gram_ref[2 * slot + part, pl.ds(member, 8, stride=4)]
                shift = (member * quarter - base) % columns
                if shift:
                    piece = pltpu.roll(piece, shift, 1)
                row = piece if row is None else jnp.where(lane_group == member, piece, row)
            out_ref[pl.ds(index * 16 + part, 8, stride=2)] = row * factor

    def degree_step(index, carry):
        place = pl.ds(index * PITCH, pairs)
        total = gram(kept_ref[place].astype(jnp.bfloat16))
        flat(total, 0, low_ref, index, factor_ref[pl.ds(index, 1)])
        total = gram(moved_ref[place].astype(jnp.bfloat16)) + gram(mirrored_ref[place].astype(jnp.bfloat16))
        flat(total, 1, mirror_ref, index, factor_ref[pl.ds(half + index, 1)])
        return carry

    lax.fori_loop(0, half, degree_step, 0, unroll=2)


def spectra_rows(start, low_orders, weight, rows, chunk, chunks, degrees):
    pairs = low_orders.shape[0]
    columns = rows.shape[1]
    half = rows.shape[0] // pairs // 2
    out = jax.ShapeDtypeStruct((half * 16, columns), jnp.float32)
    return pl.pallas_call(
        functools.partial(spectra_kernel, chunk, degrees),
        out_shape=(out, out),
        in_specs=[SMEM_SPEC, SMEM_SPEC, VMEM_SPEC, VMEM_SPEC, VMEM_SPEC],
        out_specs=(VMEM_SPEC, VMEM_SPEC),
        scratch_shapes=[
            pltpu.VMEM((half * PITCH, columns), jnp.float32),
            pltpu.VMEM((2 * half * PITCH, columns), jnp.float32),
            pltpu.VMEM((half * PITCH, columns), jnp.float32),
            pltpu.VMEM((4, 32, columns), jnp.float32),
            pltpu.VMEM((2 * half, columns), jnp.float32),
        ],
        name=f"spectra_{chunk}",
    )(start, low_orders, low_orders[None], weight, rows)


def in_degree_order(rows, columns):
    tiles = rows.reshape(-1, 8, 2, columns)
    return jnp.swapaxes(tiles, 1, 2).reshape(-1, 2, 8 * columns)


def local(sky_maps, sky_mask, pixel_counts, phi_offsets, low_orders, legendre):
    devices = lax.axis_size(BAND_SUB)
    device_index = lax.axis_index(BAND_SUB)
    degree_count = legendre.shape[1]
    rows = sky_maps.shape[1] * sky_maps.shape[2]
    columns = 2 * rows
    range_rows = degree_count // devices
    outgoing = fourier(
        sky_maps.reshape(rows, sky_maps.shape[3]), sky_mask, pixel_counts, phi_offsets, low_orders[None], degree_count
    )
    received = lax.all_to_all(
        outgoing.reshape(devices, 4, columns), BAND_SUB, split_axis=0, concat_axis=0, tiled=True
    )
    order = lax.dynamic_slice_in_dim(low_orders, device_index, 1, 0)
    alm, weight, *sends = alm_and_send(order, received.reshape(4 * devices, columns), legendre[0], CHUNKS)
    upper_device = device_index >= devices // 2
    pair_block = jnp.minimum(device_index, devices - 1 - device_index)
    start = pair_block * range_rows + upper_device.astype(jnp.int32) * (range_rows // 2)
    route = [(device, devices - 1 - device) for device in range(devices)]
    kept, swapped = [], []
    for chunk, send in enumerate(sends):
        incoming = lax.all_to_all(
            send.reshape(devices, -1, columns), BAND_SUB, split_axis=0, concat_axis=0, tiled=True
        )
        low, mirror = spectra_rows(
            start[None], low_orders, weight, incoming.reshape(-1, columns), chunk, CHUNKS, degree_count
        )
        kept.append(jnp.where(upper_device, mirror, low))
        moving = jnp.where(upper_device, low, mirror).astype(jnp.bfloat16)
        swapped.append(lax.ppermute(moving, BAND_SUB, route).astype(jnp.float32))
    spectra = jnp.concatenate(kept + swapped, axis=0)
    return (alm[None], in_degree_order(spectra, columns))


def solution(mesh):
    torus = Mesh(
        mesh.devices.reshape(mesh.shape["groups"], 8, 8, mesh.shape["sub"]),
        ("groups", "band_0", "band_1", "sub"),
    )
    in_specs = (
        P(GROUPS_BAND_SUB, None, None, None),
        P(GROUPS_BAND_SUB, None),
        P(GROUPS_BAND_SUB),
        P(GROUPS_BAND_SUB),
        P("groups"),
        P(GROUPS_BAND_SUB, None, None),
    )
    out_specs = (P(GROUPS_BAND_SUB, None, None), P(GROUPS_BAND_SUB, None, None))
    return jax.shard_map(local, mesh=torus, in_specs=in_specs, out_specs=out_specs, check_vma=False)
```

time: 154 us -> 140 us (0.909)
  local copies, waits for them, and re-layouts: 10.4 us -> 2.64 us
  matrix products: 4.9 us -> 0 us
  other arithmetic: 6.84 us -> 2.82 us
  Pallas kernels: 19.3 us -> 22.2 us
  waiting for transfers between devices: 73.7 us -> 75.3 us
    dot_general x3 -> x0, matrix products: 4.9 us -> none  [outer_totals(): jnp.einsum('slerm,slern->lemn', split_parts, split_parts, preferred_eleme...]
    select_n x2 -> x0, local copies, waits for them, and re-layouts: 2.91 us -> none  [the longest x1 1.94 us: local(): jnp.where(kept_mask[:, :, None], jnp.zeros_like(low_rows), low_rows)]
    pallas_call x2 -> x3, Pallas kernels: 19.3 us -> 22.2 us  [the longest x1 9.74 us: spectra_rows(): pl.pallas_call(functools.partial(spectra_kernel, chunk, degrees), out_sha...]
    all_to_all x2, waiting for transfers between devices: 61.9 us -> 64.5 us  [the longest x1 53.3 us: local(): lax.all_to_all(send.reshape(devices, -1, columns), BAND_SUB, split_axis=0...]
    reshape x2 -> x0, local copies, waits for them, and re-layouts: 2.42 us -> none  [scaled_spectra(): (2.0 * totals / (weight * counts)[:, None, None, None]).reshape(degrees.s...]
    slice x3 -> x0, local copies, waits for them, and re-layouts: 2.33 us -> none  [the longest x1 1.69 us: local(): mirror_rows = incoming[:, half_rows:]]
    select_n x2 -> x1, other arithmetic: 3.31 us -> 0.99 us  [local(): kept.append(jnp.where(upper_device, mirror, low))]
where the time goes in v2:
time: 140 us
  waiting for transfers between devices  75.3 us (54%)
  starting transfers between devices  34.7 us (25%)
  Pallas kernels  22.2 us (16%)
  other arithmetic  2.82 us (2%)
  local copies, waits for them, and re-layouts  2.64 us (2%)
  between operations  2.01 us (1%)
    all_to_all x1, waiting for transfers between devices, local(): lax.all_to_all(send.reshape(devices, -1, columns), BAND_SUB, split_axis=0...  53.3 us
    all_to_all x1, starting transfers between devices, local(): lax.all_to_all(outgoing.reshape(devices, 4, columns), BAND_SUB, split_axi...  26.4 us
    all_to_all x1, waiting for transfers between devices, local(): lax.all_to_all(outgoing.reshape(devices, 4, columns), BAND_SUB, split_axi...  11.1 us
    ppermute x1, waiting for transfers between devices, local(): swapped.append(lax.ppermute(moving, BAND_SUB, route).astype(jnp.float32))  10.9 us
    pallas_call x1, Pallas kernels, spectra_rows(): pl.pallas_call(functools.partial(spectra_kernel, chunk, degrees), out_sha...  9.74 us
    all_to_all x1, starting transfers between devices, local(): lax.all_to_all(send.reshape(devices, -1, columns), BAND_SUB, split_axis=0...  8.09 us
    pallas_call x1, Pallas kernels, alm_and_send(): pl.pallas_call(functools.partial(alm_kernel, chunks, height), out_shape=(...  7.77 us
    pallas_call x1, Pallas kernels, fourier(): pl.pallas_call(functools.partial(fourier_kernel, degrees), out_shape=jax....  4.69 us
  transfers between devices with their start and end apart: 3, of which 3 were waited for; matrix products, arithmetic and copies ran while one was open for 1% of the time, Pallas kernels for 0%

profile of v2, /device:TPU:514, one launch (start us, length us, event | category | flops | bytes accessed | tf_op | source)
XLA Modules:
  0.0 139.7 jit_solution(2851785996433926077)
XLA Ops:
  0.6 0.0 copy-start.2
  1.9 4.7 %fourier.1 = bf16[512,128]{1,0:T(8,128)(2,1)} custom-call(s32[1]{0:T(128)S(6)} %copy.9.count_ref, s32[1]{0:T(128)S(6)} %copy.10.offset_ref, s32[1,128]{1,0:T(1,128)} %bitcast.21, f32[1,16384]{1,0:T(1,128)} %mask_ref.1, bf16[64,16384]{1,0:T(8,128)(2,1)} %bitcast.16), custom_call_target="tpu_custom_call" | custom-call | tf_op jit(solution)/shard_map/fourier/pallas_call | solution.py:122
  6.6 26.4 %all-to-all-start = ((bf16[128,4,128]{2,1,0:T(4,128)(2,1)}), bf16[128,4,128]{2,1,0:T(4,128)(2,1)S(1)}, u32[]{:S(2)}, u32[]{:S(2)}) async-start(bf16[128,4,128]{2,1,0:T(4,128)(2,1)} %bitcast.19), calls=%async_computation | async-start | bytes 262144 | tf_op jit(solution)/shard_map/all_to_all | solution.py:326
  33.1 0.0 copy-done.2
  33.1 0.6 dynamic_slice.3.order_ref
  33.7 11.1 %all-to-all-done = bf16[128,4,128]{2,1,0:T(4,128)(2,1)S(1)} async-done(((bf16[128,4,128]{2,1,0:T(4,128)(2,1)}), bf16[128,4,128]{2,1,0:T(4,128)(2,1)S(1)}, u32[]{:S(2)}, u32[]{:S(2)}) %all-to-all-start) | async-done | bytes 131104 | tf_op jit(solution)/shard_map/all_to_all | solution.py:326
  44.9 0.0 copy-start.1
  44.9 0.7 copy-done.1
  45.5 7.8 %alm_and_send.1 = (f32[8192,128]{1,0:T(8,128)}, f32[1,128]{1,0:T(1,128)}, bf16[8192,128]{1,0:T(8,128)(2,1)}) custom-call(s32[1]{0:T(128)} %dynamic_slice.3.order_ref, bf16[512,128]{1,0:T(8,128)(2,1)} %bitcast.18, bf16[8192,256]{1,0:T(8,128)(2,1)} %bitcast.15), custom_call_target="tpu_custom_call" | custom-call | tf_op jit(solution)/shard_map/alm_and_send/pallas_call | solution.py:207
  53.3 8.1 %all-to-all-start.1 = ((bf16[128,64,128]{2,1,0:T(8,128)(2,1)}), bf16[128,64,128]{2,1,0:T(8,128)(2,1)S(1)}, u32[]{:S(2)}, u32[]{:S(2)}) async-start(bf16[128,64,128]{2,1,0:T(8,128)(2,1)} %bitcast.17), calls=%async_computation.1 | async-start | bytes 4194304 | tf_op jit(solution)/shard_map/all_to_all | solution.py:337
  61.4 53.3 %all-to-all-done.1 = bf16[128,64,128]{2,1,0:T(8,128)(2,1)S(1)} async-done(((bf16[128,64,128]{2,1,0:T(8,128)(2,1)}), bf16[128,64,128]{2,1,0:T(8,128)(2,1)S(1)}, u32[]{:S(2)}, u32[]{:S(2)}) %all-to-all-start.1) | async-done | bytes 2097184 | tf_op jit(solution)/shard_map/all_to_all | solution.py:337
  114.7 0.0 copy-start
  114.7 1.3 copy-done
  116.1 9.7 %spectra_0.1 = (f32[512,128]{1,0:T(8,128)}, f32[512,128]{1,0:T(8,128)}) custom-call(s32[1]{0:T(128)} %bitcast.6.start_ref, s32[128]{0:T(128)} %order_ref.1, s32[1,128]{1,0:T(1,128)} %bitcast.22, f32[1,128]{1,0:T(1,128)} %get-tuple-element.8.weight_ref, bf16[8192,128]{1,0:T(8,128)(2,1)} %bitcast.14), custom_call_target="tpu_custom_call" | custom-call | tf_op jit(solution)/shard_map/spectra_0/pallas_call | solution.py:295
  125.8 1.0 select_convert_fusion
  126.8 0.1 collective-permute-start
  126.9 1.0 broadcast_select_fusion
  127.9 10.9 %collective-permute-done = bf16[512,128]{1,0:T(8,128)(2,1)S(1)} collective-permute-done((bf16[512,128]{1,0:T(8,128)(2,1)S(1)}, bf16[512,128]{1,0:T(8,128)(2,1)S(1)}, u32[]{:S(2)}, u32[]{:S(2)}) %collective-permute-start) | collective-permute-done | bytes 131104 | tf_op jit(solution)/shard_map/ppermute | solution.py:345
  138.8 0.8 pad_maximum_fusion
  (1 shorter events, 0.0 us)
Async XLA Ops:
  0.6 32.4 %copy-start.2 = (s32[128]{0:T(128)S(1)}, s32[128]{0:T(128)}, u32[]{:S(2)}) copy-start(s32[128]{0:T(128)} %order_ref.1) | copy-start | bytes 1540
  6.6 38.2 %all-to-all-start = ((bf16[128,4,128]{2,1,0:T(4,128)(2,1)}), bf16[128,4,128]{2,1,0:T(4,128)(2,1)S(1)}, u32[]{:S(2)}, u32[]{:S(2)}) async-start(bf16[128,4,128]{2,1,0:T(4,128)(2,1)} %bitcast.19), calls=%async_computation | async-start | bytes 262144 | tf_op jit(solution)/shard_map/all_to_all | solution.py:326
  44.9 0.7 copy-start.1
  53.3 61.4 %all-to-all-start.1 = ((bf16[128,64,128]{2,1,0:T(8,128)(2,1)}), bf16[128,64,128]{2,1,0:T(8,128)(2,1)S(1)}, u32[]{:S(2)}, u32[]{:S(2)}) async-start(bf16[128,64,128]{2,1,0:T(8,128)(2,1)} %bitcast.17), calls=%async_computation.1 | async-start | bytes 4194304 | tf_op jit(solution)/shard_map/all_to_all | solution.py:337
  114.7 1.3 copy-start
  126.8 12.0 %collective-permute-start = (bf16[512,128]{1,0:T(8,128)(2,1)S(1)}, bf16[512,128]{1,0:T(8,128)(2,1)S(1)}, u32[]{:S(2)}, u32[]{:S(2)}) collective-permute-start(bf16[512,128]{1,0:T(8,128)(2,1)S(1)} %select_convert_fusion), channel_id=1, source_target_pairs={{0,127},{1,126},{2,125},{3,124},{4,123},{5,122},{6,121},{7,120},{8... | collective-permute-start | bytes 393224 | tf_op jit(solution)/shard_map/ppermute | solution.py:345

commit v3 on v2

v3 whole, which is shorter than its diff:
```python
import functools

import jax
import jax.numpy as jnp
from jax import lax
from jax.experimental import pallas as pl
from jax.experimental.pallas import tpu as pltpu
from jax.sharding import Mesh
from jax.sharding import PartitionSpec as P

BAND_SUB = ("band_0", "band_1", "sub")
GROUPS_BAND_SUB = ("groups", "band_0", "band_1", "sub")

FINE = 256
GROUP = 8
PITCH = 132
READS = 2
PIECES = 2
MAP_READS = 2
SLOTS = 16
GRAMS = 16
PARTS = 4
UNROLL = 4
VMEM_LIMIT = 67043328
VMEM_SPEC = pl.BlockSpec(memory_space=pltpu.VMEM)
SMEM_SPEC = pl.BlockSpec(memory_space=pltpu.SMEM)
HBM_SPEC = pl.BlockSpec(memory_space=pltpu.HBM)


def mod_units(units, modulus, inverse):
    quotient = jnp.floor(units.astype(jnp.float32) * inverse).astype(jnp.int32)
    rest = units - quotient * modulus
    rest = jnp.where(rest < 0, rest + modulus, rest)
    return jnp.where(rest >= modulus, rest - modulus, rest)


def turn(units, modulus, inverse, scale):
    angle = scale * mod_units(units, modulus, inverse).astype(jnp.float32)
    return jnp.cos(angle), jnp.sin(angle)


def combine(first, second):
    (a_cos, a_sin), (b_cos, b_sin) = first, second
    return a_cos * b_cos - a_sin * b_sin, a_sin * b_cos + a_cos * b_sin


def fourier_kernel(
    degrees, count_ref, offset_ref, order_hbm, mask_hbm, maps_hbm, out_ref, table_ref, outer_ref, rows_ref, join_ref,
    maps_ref, sems, order_ref, mask_ref, small_sems,
):
    small = [
        pltpu.make_async_copy(source, target, small_sems.at[index])
        for index, (source, target) in enumerate(((order_hbm, order_ref), (mask_hbm, mask_ref)))
    ]
    for copy in small:
        copy.start()
    width = maps_hbm.shape[1] // sems.shape[0]
    copies = []
    for group in range(sems.shape[0]):
        place = pl.ds(group * width, width)
        copy = pltpu.make_async_copy(maps_hbm.at[:, place], maps_ref.at[:, place], sems.at[group])
        copy.start()
        copies.append(copy)
    pixel_slots = maps_ref.shape[1]
    rows = maps_ref.shape[0]
    maps_count = rows // 2
    pairs = order_ref.shape[1]
    slots = 2 * pairs
    for copy in small:
        copy.wait()
    count = count_ref[0]
    offset = offset_ref[0]
    count_float = count.astype(jnp.float32)
    modulus = 2 * count
    inverse = 1.0 / modulus.astype(jnp.float32)
    scale = jnp.pi / count_float
    low_orders = order_ref[...]
    orders = jnp.concatenate([low_orders, degrees - low_orders], axis=1)
    twice = 2 * orders
    coarse = pixel_slots // FINE
    near = 16
    step = lax.broadcasted_iota(jnp.int32, (near, slots), 0)
    low = turn(twice * step, modulus, inverse, scale)
    high = turn(twice * (near * step), modulus, inverse, scale)
    for index in range(FINE // near):
        here = tuple(part[index : index + 1] for part in high)
        cosine, sine = combine(here, low)
        table_ref[near * index : near * (index + 1), :slots] = cosine.astype(jnp.bfloat16)
        table_ref[near * index : near * (index + 1), slots:] = sine.astype(jnp.bfloat16)
    step = lax.broadcasted_iota(jnp.int32, (8, slots), 0)
    low = turn(twice * (FINE * step) + orders * offset, modulus, inverse, scale)
    high = turn(twice * (8 * FINE * step), modulus, inverse, scale)
    for index in range(coarse // 8):
        here = tuple(part[index : index + 1] for part in high)
        cosine, sine = combine(here, low)
        outer_ref[8 * index : 8 * (index + 1), :slots] = cosine
        outer_ref[8 * index : 8 * (index + 1), slots:] = sine
    pixels = lax.broadcasted_iota(jnp.int32, (1, pixel_slots), 1)
    mask = jnp.where(pixels < count, mask_ref[...], 0.0)
    square = jnp.sum(mask * mask)
    table = table_ref[...]
    real_sum = jnp.zeros((rows, slots), jnp.float32)
    imag_sum = jnp.zeros((rows, slots), jnp.float32)
    for group in range(coarse // GROUP):
        if group * GROUP * FINE % width == 0:
            copies[group * GROUP * FINE // width].wait()
        buffer = rows_ref.at[group % 2]
        for member in range(GROUP):
            first = (group * GROUP + member) * FINE
            block = maps_ref[:, first : first + FINE].astype(jnp.float32) * mask[:, first : first + FINE]
            buffer[member * rows : (member + 1) * rows, :] = block.astype(jnp.bfloat16)
        inner = jnp.dot(buffer[...], table, preferred_element_type=jnp.float32)
        for member in range(GROUP):
            index = group * GROUP + member
            cosine = outer_ref[index : index + 1, :slots]
            sine = outer_ref[index : index + 1, slots:]
            inner_cos = inner[member * rows : (member + 1) * rows, :slots]
            inner_sin = inner[member * rows : (member + 1) * rows, slots:]
            real_sum = real_sum + (cosine * inner_cos - sine * inner_sin)
            imag_sum = imag_sum + (sine * inner_cos + cosine * inner_sin)
    inverse_root = 1.0 / jnp.sqrt(count_float)
    live = twice < count
    real_part = jnp.where(live, real_sum * inverse_root, 0.0)
    imag_part = jnp.where(live, -imag_sum * inverse_root, 0.0)
    joined = jnp.concatenate(
        [real_part[:maps_count], imag_part[:maps_count], real_part[maps_count:], imag_part[maps_count:]], axis=0
    )
    join_ref[pl.ds(0, pairs, stride=4)] = jnp.transpose(joined[:, :pairs])
    join_ref[pl.ds(1, pairs, stride=4)] = jnp.transpose(joined[:, pairs:])
    lane = lax.broadcasted_iota(jnp.int32, (1, 2 * rows), 1)
    value = jnp.where(lane < 3, square, count_float)
    top = value.astype(jnp.bfloat16).astype(jnp.float32)
    middle = (value - top).astype(jnp.bfloat16).astype(jnp.float32)
    bottom = ((value - top) - middle).astype(jnp.bfloat16).astype(jnp.float32)
    kind = lane % 3
    pieces = jnp.where(kind == 0, top, jnp.where(kind == 1, middle, bottom))
    pieces = jnp.broadcast_to(jnp.where(lane < 6, pieces, 0.0), (pairs, 2 * rows))
    join_ref[pl.ds(2, pairs, stride=4)] = pieces
    join_ref[pl.ds(3, pairs, stride=4)] = pieces
    out_ref[...] = join_ref[...].astype(jnp.bfloat16)


def fourier(maps, mask, count, offset, low_orders, degrees):
    rows, pixel_slots = maps.shape
    pairs = low_orders.shape[1]
    slots = 2 * pairs
    return pl.pallas_call(
        functools.partial(fourier_kernel, degrees),
        out_shape=jax.ShapeDtypeStruct((4 * pairs, 2 * rows), jnp.bfloat16),
        in_specs=[SMEM_SPEC] * 2 + [HBM_SPEC] * 3,
        out_specs=VMEM_SPEC,
        scratch_shapes=[
            pltpu.VMEM((FINE, 2 * slots), jnp.bfloat16),
            pltpu.VMEM((pixel_slots // FINE, 2 * slots), jnp.float32),
            pltpu.VMEM((2, GROUP * rows, FINE), jnp.bfloat16),
            pltpu.VMEM((4 * pairs, 2 * rows), jnp.float32),
            pltpu.VMEM((rows, pixel_slots), jnp.bfloat16),
            pltpu.SemaphoreType.DMA((MAP_READS,)),
            pltpu.VMEM((1, pairs), jnp.int32),
            pltpu.VMEM((1, pixel_slots), jnp.float32),
            pltpu.SemaphoreType.DMA((2,)),
        ],
        name="fourier",
    )(count, offset, low_orders, mask, maps)


def plan_kernel(range_rows, device_ref, orders_ref, plan_ref):
    device = device_ref[0]
    devices = orders_ref.shape[0]
    upper = (device >= devices // 2).astype(jnp.int32)
    plan_ref[0] = orders_ref[device]
    plan_ref[1] = jnp.minimum(device, devices - 1 - device) * range_rows + upper * (range_rows // 2)
    plan_ref[2] = upper


def plan_of(device, low_orders, range_rows):
    return pl.pallas_call(
        functools.partial(plan_kernel, range_rows),
        out_shape=jax.ShapeDtypeStruct((3,), jnp.int32),
        in_specs=[SMEM_SPEC, SMEM_SPEC],
        out_specs=SMEM_SPEC,
        compiler_params=pltpu.CompilerParams(vmem_limit_bytes=VMEM_LIMIT),
        name="plan",
    )(device, low_orders)


def make_operands(given32_ref, operand_ref):
    columns = given32_ref.shape[1]
    cycles = given32_ref.shape[0] // 4
    quarter = columns // 4
    row = lax.broadcasted_iota(jnp.int32, (columns, columns), 0)
    column = lax.broadcasted_iota(jnp.int32, (columns, columns), 1)
    part = column // quarter
    hit = (row // quarter == 3 - part) & (row % quarter == column % quarter)
    sign = jnp.where((part == 1) | (part == 2), -1.0, 1.0)
    swap = jnp.where(hit, sign, 0.0).astype(jnp.bfloat16)
    for slot in range(2):
        block = given32_ref[pl.ds(slot, cycles, stride=4)].astype(jnp.bfloat16)
        lower = jnp.dot(block, swap, preferred_element_type=jnp.float32)
        operand_ref[slot, :cycles] = -block
        operand_ref[slot, cycles:] = (-lower).astype(jnp.bfloat16)


def alm_products(split, legendre_hbm, legendre_ref, operand_ref, held_ref, pad, height, sems):
    degrees = legendre_ref.shape[0]
    reads = sems.shape[0]
    for tile in range(degrees // height):
        first_row = tile * height
        place = pl.ds(first_row, height)
        if first_row % (degrees // reads) == 0:
            legendre_read(legendre_hbm, legendre_ref, sems, first_row * reads // degrees).wait()
        slot = (first_row >= split).astype(jnp.int32)
        held_ref[pad + first_row : pad + first_row + height] = jnp.dot(
            legendre_ref[place], operand_ref[slot], preferred_element_type=jnp.float32
        )
    border = pl.multiple_of(split // height * height, height)
    other = jnp.dot(legendre_ref[pl.ds(border, height)], operand_ref[1], preferred_element_type=jnp.float32)
    row_index = border + lax.broadcasted_iota(jnp.int32, (height, 1), 0)
    place = pl.ds(pad + border, height)
    held_ref[place] = jnp.where(row_index >= split, other, held_ref[place])


def legendre_read(legendre_hbm, legendre_ref, sems, part):
    size = legendre_ref.shape[0] // sems.shape[0]
    place = pl.ds(part * size, size)
    return pltpu.make_async_copy(legendre_hbm.at[place], legendre_ref.at[place], sems.at[part])


def send_kernel(
    height, plan_hbm, given_hbm, legendre_hbm, send_hbm,
    given_ref, given32_ref, operand_ref, held_ref, legendre_ref, send_ref, sems, send_sems, given_sem, plan_ref, plan_sem,
):
    plan_read = pltpu.make_async_copy(plan_hbm, plan_ref, plan_sem)
    plan_read.start()
    given_read = pltpu.make_async_copy(given_hbm, given_ref, given_sem)
    given_read.start()
    for part in range(sems.shape[0]):
        legendre_read(legendre_hbm, legendre_ref, sems, part).start()
    cycles = given_ref.shape[0] // 4
    degrees = legendre_ref.shape[0]
    plan_read.wait()
    order = plan_ref[0]
    given_read.wait()
    given32_ref[...] = given_ref[...].astype(jnp.float32)
    make_operands(given32_ref, operand_ref)
    alm_products(degrees - order, legendre_hbm, legendre_ref, operand_ref, held_ref, 32, height, sems)

    half = degrees // cycles // 2
    step = lax.broadcasted_iota(jnp.int32, (half, 1), 0)
    batch = cycles // send_sems.shape[0]
    for piece in range(send_sems.shape[0]):
        upper = piece * batch >= cycles // 2

        def one(index, carry, piece=piece, upper=upper):
            device = piece * batch + index
            block = cycles - 1 - device if upper else device
            start = pl.multiple_of(device * 2 * half, 2 * half)
            low = 2 * half * block + (half if upper else 0)
            kept = held_ref[pl.ds(32 + jnp.maximum(low - order, -half), half)]
            moved = held_ref[pl.ds(32 + degrees - jnp.minimum(low + half, order), half)]
            mirror = held_ref[pl.ds(32 + degrees - half - low - order, half)]
            mixed = jnp.where(step >= order - low, kept, moved)
            send_ref[pl.ds(start, half)] = mixed.astype(jnp.bfloat16)
            send_ref[pl.ds(start + half, half)] = mirror.astype(jnp.bfloat16)
            return carry

        lax.fori_loop(0, batch, one, 0, unroll=4)
        place = pl.ds(piece * batch * 2 * half, batch * 2 * half)
        pltpu.make_async_copy(send_ref.at[place], send_hbm.at[place], send_sems.at[piece]).start()
    for piece in range(send_sems.shape[0]):
        place = pl.ds(piece * batch * 2 * half, batch * 2 * half)
        pltpu.make_async_copy(send_ref.at[place], send_hbm.at[place], send_sems.at[piece]).wait()


def rows_to_send(plan, given, legendre, height=512):
    degrees, inner = legendre.shape
    columns = given.shape[1]
    return pl.pallas_call(
        functools.partial(send_kernel, height),
        out_shape=jax.ShapeDtypeStruct((degrees, columns), jnp.bfloat16),
        in_specs=[HBM_SPEC] * 3,
        out_specs=HBM_SPEC,
        scratch_shapes=[
            pltpu.VMEM(given.shape, jnp.bfloat16),
            pltpu.VMEM(given.shape, jnp.float32),
            pltpu.VMEM((2, inner, columns), jnp.bfloat16),
            pltpu.VMEM((degrees + 64, columns), jnp.float32),
            pltpu.VMEM((degrees, inner), jnp.bfloat16),
            pltpu.VMEM((degrees, columns), jnp.bfloat16),
            pltpu.SemaphoreType.DMA((READS,)),
            pltpu.SemaphoreType.DMA((PIECES,)),
            pltpu.SemaphoreType.DMA,
            pltpu.SMEM(plan.shape, jnp.int32),
            pltpu.SemaphoreType.DMA,
        ],
        name="rows_to_send",
    )(plan, given, legendre)


def alm_kernel(
    height, plan_ref, given_ref, legendre_hbm, alm_hbm, weight_ref, given32_ref, operand_ref, held_ref, legendre_ref, sems, sem
):
    for part in range(sems.shape[0]):
        legendre_read(legendre_hbm, legendre_ref, sems, part).start()
    given32_ref[...] = given_ref[...].astype(jnp.float32)
    make_operands(given32_ref, operand_ref)
    cycles = given_ref.shape[0] // 4
    pieces = given32_ref[pl.ds(2, cycles, stride=4)]
    lane = lax.broadcasted_iota(jnp.int32, pieces.shape, 1)
    square = jnp.sum(jnp.where(lane < 3, pieces, 0.0))
    pixels = jnp.sum(jnp.where(lane < 3, 0.0, pieces))
    weight_ref[...] = jnp.full(weight_ref.shape, square / pixels, jnp.float32)
    split = legendre_ref.shape[0] - plan_ref[0]
    alm_products(split, legendre_hbm, legendre_ref, operand_ref, held_ref, 0, height, sems)
    copy = pltpu.make_async_copy(held_ref, alm_hbm, sem)
    copy.start()
    copy.wait()


def packed_alm(plan, given, legendre, height=512):
    degrees, inner = legendre.shape
    columns = given.shape[1]
    return pl.pallas_call(
        functools.partial(alm_kernel, height),
        out_shape=(
            jax.ShapeDtypeStruct((degrees, columns), jnp.float32),
            jax.ShapeDtypeStruct((1, columns), jnp.float32),
        ),
        in_specs=[SMEM_SPEC, VMEM_SPEC, HBM_SPEC],
        out_specs=(HBM_SPEC, VMEM_SPEC),
        scratch_shapes=[
            pltpu.VMEM(given.shape, jnp.float32),
            pltpu.VMEM((2, inner, columns), jnp.bfloat16),
            pltpu.VMEM((degrees, columns), jnp.float32),
            pltpu.VMEM((degrees, inner), jnp.bfloat16),
            pltpu.SemaphoreType.DMA((READS,)),
            pltpu.SemaphoreType.DMA,
        ],
        compiler_params=pltpu.CompilerParams(vmem_limit_bytes=VMEM_LIMIT),
        name="packed_alm",
    )(plan, given, legendre)


def spectra_kernel(
    travels, degrees, plan_hbm, orders_hbm, order_row_hbm, weight_hbm, rows_hbm, out_ref,
    rows_ref, first_ref, second_ref, gram_ref, factor_ref, total_ref, sems, out_sem,
    plan_ref, order_ref, order_row_ref, weight_ref, small_sems,
):
    small = [
        pltpu.make_async_copy(source, target, small_sems.at[index])
        for index, (source, target) in enumerate(
            ((plan_hbm, plan_ref), (orders_hbm, order_ref), (order_row_hbm, order_row_ref), (weight_hbm, weight_ref))
        )
    ]
    for copy in small:
        copy.start()
    pairs = order_row_ref.shape[1]
    half = rows_ref.shape[0] // pairs // 2
    parts = sems.shape[0]
    height = rows_ref.shape[0] // parts

    def reading(part):
        place = pl.ds(part * height, height)
        return pltpu.make_async_copy(rows_hbm.at[place], rows_ref.at[place], sems.at[part])

    for part in range(parts):
        reading(part).start()
    for copy in small:
        copy.wait()
    first = plan_ref[1]
    upper = plan_ref[2] == 1
    low_wanted = upper if travels else jnp.logical_not(upper)
    step = lax.broadcasted_iota(jnp.int32, (half, 1), 0)
    columns = rows_ref.shape[1]
    quarter = columns // 4

    degree = jnp.where(low_wanted, first, degrees - half - first) + step
    orders = order_row_ref[...]
    below = (orders <= degree).astype(jnp.float32) + (degrees - orders <= degree).astype(jnp.float32)
    counts = jnp.maximum(jnp.sum(below, axis=1, keepdims=True), 1.0)
    factor_ref[...] = 2.0 / (weight_ref[...] * counts)

    def block_of(pair):
        start = pl.multiple_of(pair * 2 * half, 2 * half)
        return rows_ref[pl.ds(start, 2 * half)].astype(jnp.float32)

    def keep(pair, carry):
        early = order_ref[pair] - first
        block = jnp.where(step >= early, block_of(pair)[:half], 0.0)
        first_ref[pl.ds(pair, half, stride=PITCH)] = block
        return carry

    def move(pair, carry):
        block = block_of(pair)
        early = jnp.clip(order_ref[pair] - first, 0, half)
        first_ref[pl.ds((half - early) * PITCH + pair, half, stride=PITCH)] = block[:half]
        second_ref[pl.ds(pair, half, stride=PITCH)] = block[half:]
        return carry

    def place_rows(body):
        for part in range(parts):
            reading(part).wait()
            lax.fori_loop(part * (pairs // parts), (part + 1) * (pairs // parts), body, 0, unroll=UNROLL)

    def gram(rows):
        return lax.dot_general(rows, rows, (((0,), (0,)), ((), ())), preferred_element_type=jnp.float32)

    lane_group = lax.broadcasted_iota(jnp.int32, (8, columns), 1) // quarter

    def fold(total, index):
        for part in range(2):
            base = 2 * part * quarter
            real = total[base : base + quarter]
            imag = total[base + quarter : base + 2 * quarter]
            gram_ref[2 * index + part] = real + pltpu.roll(imag, columns - quarter, 1)

    def write_rows(step_index, carry):
        for slot in range(SLOTS):
            index = SLOTS * step_index + slot
            factor = factor_ref[pl.ds(index, 1)]
            for part in range(2):
                row = None
                for member in range(4):
                    piece = gram_ref[2 * index + part, pl.ds(member, 8, stride=4)]
                    shift = (member - 2 * part) * quarter % columns
                    if shift:
                        piece = pltpu.roll(piece, shift, 1)
                    row = piece if row is None else jnp.where(lane_group == member, piece, row)
                total_ref[pl.ds(index * 16 + part, 8, stride=2)] = row * factor
        return carry

    @pl.when(low_wanted)
    def _():
        place_rows(keep)

        def degree_step(index, carry):
            for slot in range(GRAMS):
                here = GRAMS * index + slot
                rows = first_ref[pl.ds(here * PITCH, pairs)].astype(jnp.bfloat16)
                fold(gram(rows), here)
            return carry

        lax.fori_loop(0, half // GRAMS, degree_step, 0)

    @pl.when(jnp.logical_not(low_wanted))
    def _():
        first_ref[0 : half * PITCH] = jnp.zeros((half * PITCH, columns), jnp.float32)
        place_rows(move)

        def degree_step(index, carry):
            for slot in range(GRAMS):
                here = GRAMS * index + slot
                place = pl.ds(here * PITCH, pairs)
                moved = first_ref[place].astype(jnp.bfloat16)
                mirrored = second_ref[place].astype(jnp.bfloat16)
                fold(gram(moved) + gram(mirrored), here)
            return carry

        lax.fori_loop(0, half // GRAMS, degree_step, 0)

    lax.fori_loop(0, half // SLOTS, write_rows, 0)
    if travels:
        out_ref[...] = total_ref[...].astype(out_ref.dtype)
    else:
        copy = pltpu.make_async_copy(total_ref, out_ref.at[pl.ds(0, total_ref.shape[0])], out_sem)
        copy.start()
        copy.wait()


def spectra_rows(plan, low_orders, weight, rows, travels, degrees):
    pairs = low_orders.shape[0]
    columns = rows.shape[1]
    half = rows.shape[0] // pairs // 2
    out = jax.ShapeDtypeStruct((half * (16 if travels else 32), columns), jnp.bfloat16 if travels else jnp.float32)
    return pl.pallas_call(
        functools.partial(spectra_kernel, travels, degrees),
        out_shape=out,
        in_specs=[HBM_SPEC] * 5,
        out_specs=VMEM_SPEC if travels else HBM_SPEC,
        scratch_shapes=[
            pltpu.VMEM(rows.shape, jnp.bfloat16),
            pltpu.VMEM((2 * half * PITCH, columns), jnp.float32),
            pltpu.VMEM((half * PITCH, columns), jnp.float32),
            pltpu.VMEM((2 * half, 32, columns), jnp.float32),
            pltpu.VMEM((half, columns), jnp.float32),
            pltpu.VMEM((half * 16, columns), jnp.float32),
            pltpu.SemaphoreType.DMA((PARTS,)),
            pltpu.SemaphoreType.DMA,
            pltpu.SMEM(plan.shape, jnp.int32),
            pltpu.SMEM(low_orders.shape, jnp.int32),
            pltpu.VMEM((1, pairs), jnp.int32),
            pltpu.VMEM(weight.shape, jnp.float32),
            pltpu.SemaphoreType.DMA((4,)),
        ],
        name="spectra_travel" if travels else "spectra_stay",
    )(plan, low_orders, low_orders[None], weight, rows)


def in_degree_order(rows, columns):
    tiles = rows.reshape(-1, 8, 2, columns)
    return jnp.swapaxes(tiles, 1, 2).reshape(-1, 2, 8 * columns)


def local(sky_maps, sky_mask, pixel_counts, phi_offsets, low_orders, legendre):
    devices = lax.axis_size(BAND_SUB)
    device_index = lax.axis_index(BAND_SUB)
    degree_count = legendre.shape[1]
    rows = sky_maps.shape[1] * sky_maps.shape[2]
    columns = 2 * rows
    range_rows = degree_count // devices
    outgoing = fourier(
        sky_maps.reshape(rows, sky_maps.shape[3]), sky_mask, pixel_counts, phi_offsets, low_orders[None], degree_count
    )
    received = lax.all_to_all(
        outgoing.reshape(devices, 4, columns), BAND_SUB, split_axis=0, concat_axis=0, tiled=True
    ).reshape(4 * devices, columns)
    plan = plan_of(device_index[None], low_orders, range_rows)
    send = rows_to_send(plan, received, legendre[0])
    incoming = lax.all_to_all(
        send.reshape(devices, range_rows, columns), BAND_SUB, split_axis=0, concat_axis=0, tiled=True
    ).reshape(-1, columns)
    alm, weight = packed_alm(plan, received, legendre[0])
    route = [(device, devices - 1 - device) for device in range(devices)]
    moving = spectra_rows(plan, low_orders, weight, incoming, True, degree_count)
    swapped = lax.ppermute(moving, BAND_SUB, route)
    kept = spectra_rows(plan, low_orders, weight, incoming, False, degree_count)
    spectra = lax.dynamic_update_slice_in_dim(kept, swapped.astype(jnp.float32), swapped.shape[0], 0)
    return (alm[None], in_degree_order(spectra, columns))


def solution(mesh):
    torus = Mesh(
        mesh.devices.reshape(mesh.shape["groups"], 8, 8, mesh.shape["sub"]),
        ("groups", "band_0", "band_1", "sub"),
    )
    in_specs = (
        P(GROUPS_BAND_SUB, None, None, None),
        P(GROUPS_BAND_SUB, None),
        P(GROUPS_BAND_SUB),
        P(GROUPS_BAND_SUB),
        P("groups"),
        P(GROUPS_BAND_SUB, None, None),
    )
    out_specs = (P(GROUPS_BAND_SUB, None, None), P(GROUPS_BAND_SUB, None, None))
    return jax.shard_map(local, mesh=torus, in_specs=in_specs, out_specs=out_specs, check_vma=False)
```

time: 140 us -> 130 us (0.929)
  waiting for transfers between devices: 75.3 us -> 65.8 us
  Pallas kernels: 22.2 us -> 25.4 us
  local copies, waits for them, and re-layouts: 2.64 us -> 0 us
  other arithmetic: 2.82 us -> 0.72 us
    all_to_all x1, waiting for transfers between devices: 53.3 us -> 46.7 us  [local(): lax.all_to_all(send.reshape(devices, range_rows, columns), BAND_SUB, spli...]
    pallas_call x2 -> x5, Pallas kernels: 17.5 us -> 21 us  [the longest x2 7.83 us: spectra_rows(): pl.pallas_call(functools.partial(spectra_kernel, travels, degrees), out_s...]
    ppermute x1, waiting for transfers between devices: 10.9 us -> 8.44 us  [local(): swapped = lax.ppermute(moving, BAND_SUB, route)]
    unnamed x6 -> x0, local copies, waits for them, and re-layouts: 2 us -> none
  transfers between devices with their start and end apart: 3 -> 3, of which waited for: 3 -> 3; matrix products, arithmetic and copies ran while one was open for 1% -> 0% of each run, Pallas kernels for 0% -> 9%
where the time goes in v3:
time: 130 us
  waiting for transfers between devices  65.8 us (51%)
  starting transfers between devices  36 us (28%)
  Pallas kernels  25.4 us (20%)
  between operations  2 us (2%)
    all_to_all x1, waiting for transfers between devices, local(): lax.all_to_all(send.reshape(devices, range_rows, columns), BAND_SUB, spli...  46.7 us
    all_to_all x1, starting transfers between devices, local(): lax.all_to_all(outgoing.reshape(devices, 4, columns), BAND_SUB, split_axi...  27 us
    all_to_all x1, waiting for transfers between devices, local(): lax.all_to_all(outgoing.reshape(devices, 4, columns), BAND_SUB, split_axi...  10.7 us
    all_to_all x1, starting transfers between devices, local(): lax.all_to_all(send.reshape(devices, range_rows, columns), BAND_SUB, spli...  8.78 us
    ppermute x1, waiting for transfers between devices, local(): swapped = lax.ppermute(moving, BAND_SUB, route)  8.44 us
    pallas_call x2, Pallas kernels, spectra_rows(): pl.pallas_call(functools.partial(spectra_kernel, travels, degrees), out_s...  7.83 us
    pallas_call x1, Pallas kernels, packed_alm(): pl.pallas_call(functools.partial(alm_kernel, height), out_shape=(jax.Shap...  6.65 us
    pallas_call x1, Pallas kernels, rows_to_send(): pl.pallas_call(functools.partial(send_kernel, height), out_shape=jax.Shap...  5.32 us
  transfers between devices with their start and end apart: 3, of which 3 were waited for; matrix products, arithmetic and copies ran while one was open for 0% of the time, Pallas kernels for 9%

profile of v3, /device:TPU:514, one launch (start us, length us, event | category | flops | bytes accessed | tf_op | source)
XLA Modules:
  0.0 129.9 jit_solution(5915413899149234350)
XLA Ops:
  1.9 4.4 %fourier.1 = bf16[512,128]{1,0:T(8,128)(2,1)} custom-call(s32[1]{0:T(128)S(6)} %copy.10.count_ref, s32[1]{0:T(128)S(6)} %copy.11.offset_ref, s32[1,128]{1,0:T(1,128)} %bitcast.20, f32[1,16384]{1,0:T(1,128)} %mask_hbm.1, bf16[64,16384]{1,0:T(8,128)(2,1)} %bitcast.17), custom_call_target="tpu_custom_call" | custom-call | tf_op jit(solution)/shard_map/fourier/pallas_call | solution.py:147
  6.3 27.0 %all-to-all-start = ((bf16[128,4,128]{2,1,0:T(4,128)(2,1)}), bf16[128,4,128]{2,1,0:T(4,128)(2,1)}, u32[]{:S(2)}, u32[]{:S(2)}) async-start(bf16[128,4,128]{2,1,0:T(4,128)(2,1)} %bitcast.18), calls=%async_computation | async-start | bytes 262144 | tf_op jit(solution)/shard_map/all_to_all | solution.py:514
  33.3 1.2 plan.1.plan_ref.plan_hbm
  34.5 10.7 %all-to-all-done = bf16[128,4,128]{2,1,0:T(4,128)(2,1)} async-done(((bf16[128,4,128]{2,1,0:T(4,128)(2,1)}), bf16[128,4,128]{2,1,0:T(4,128)(2,1)}, u32[]{:S(2)}, u32[]{:S(2)}) %all-to-all-start) | async-done | bytes 131104 | tf_op jit(solution)/shard_map/all_to_all | solution.py:514
  45.2 5.3 %rows_to_send.1 = bf16[8192,128]{1,0:T(8,128)(2,1)} custom-call(s32[3]{0:T(128)} %plan.1.plan_ref.plan_hbm, bf16[512,128]{1,0:T(8,128)(2,1)} %bitcast.4.given_ref.given_hbm, bf16[8192,256]{1,0:T(8,128)(2,1)} %bitcast.14), custom_call_target="tpu_custom_call" | custom-call | tf_op jit(solution)/shard_map/rows_to_send/pallas_call | solution.py:278
  50.6 8.8 %all-to-all-start.1 = ((bf16[128,64,128]{2,1,0:T(8,128)(2,1)}), bf16[128,64,128]{2,1,0:T(8,128)(2,1)}, u32[]{:S(2)}, u32[]{:S(2)}) async-start(bf16[128,64,128]{2,1,0:T(8,128)(2,1)} %bitcast.16), calls=%async_computation.1 | async-start | bytes 4194304 | tf_op jit(solution)/shard_map/all_to_all | solution.py:519
  59.4 6.7 %packed_alm.1 = (f32[8192,128]{1,0:T(8,128)}, f32[1,128]{1,0:T(1,128)}) custom-call(s32[3]{0:T(128)} %plan.1.plan_ref.plan_hbm, bf16[512,128]{1,0:T(8,128)(2,1)} %bitcast.4.given_ref.given_hbm, bf16[8192,256]{1,0:T(8,128)(2,1)} %bitcast.15), custom_call_target="tpu_custom_call" | custom-call | tf_op jit(solution)/shard_map/packed_alm/pallas_call | solution.py:323
  66.0 46.7 %all-to-all-done.1 = bf16[128,64,128]{2,1,0:T(8,128)(2,1)} async-done(((bf16[128,64,128]{2,1,0:T(8,128)(2,1)}), bf16[128,64,128]{2,1,0:T(8,128)(2,1)}, u32[]{:S(2)}, u32[]{:S(2)}) %all-to-all-start.1) | async-done | bytes 2097184 | tf_op jit(solution)/shard_map/all_to_all | solution.py:519
  112.7 4.2 %spectra_travel.1 = bf16[512,128]{1,0:T(8,128)(2,1)} custom-call(s32[3]{0:T(128)} %plan.1.plan_ref.plan_hbm, s32[128]{0:T(128)} %orders_hbm.3, s32[1,128]{1,0:T(1,128)} %bitcast.21, f32[1,128]{1,0:T(1,128)} %get-tuple-element.5.weight_hbm, bf16[8192,128]{1,0:T(8,128)(2,1)} %bitcast.8.rows_hbm), custom_call_target="tpu_custom_call" | custom-call | tf_op jit(solution)/shard_map/spectra_travel/pallas_call | solution.py:475
  116.9 0.1 collective-permute-start
  117.1 3.6 %spectra_stay.1 = f32[1024,128]{1,0:T(8,128)} custom-call(s32[3]{0:T(128)} %plan.1.plan_ref.plan_hbm, s32[128]{0:T(128)} %orders_hbm.3, s32[1,128]{1,0:T(1,128)} %bitcast.22, f32[1,128]{1,0:T(1,128)} %get-tuple-element.5.weight_hbm, bf16[8192,128]{1,0:T(8,128)(2,1)} %bitcast.8.rows_hbm), custom_call_target="tpu_custom_call" | custom-call | tf_op jit(solution)/shard_map/spectra_stay/pallas_call | solution.py:475
  120.7 8.4 %collective-permute-done = bf16[512,128]{1,0:T(8,128)(2,1)S(1)} collective-permute-done((bf16[512,128]{1,0:T(8,128)(2,1)}, bf16[512,128]{1,0:T(8,128)(2,1)S(1)}, u32[]{:S(2)}, u32[]{:S(2)}) %collective-permute-start) | collective-permute-done | bytes 131104 | tf_op jit(solution)/shard_map/ppermute | solution.py:525
  129.2 0.7 convert_dynamic-update-slice_fusion
Async XLA Ops:
  6.3 38.9 %all-to-all-start = ((bf16[128,4,128]{2,1,0:T(4,128)(2,1)}), bf16[128,4,128]{2,1,0:T(4,128)(2,1)}, u32[]{:S(2)}, u32[]{:S(2)}) async-start(bf16[128,4,128]{2,1,0:T(4,128)(2,1)} %bitcast.18), calls=%async_computation | async-start | bytes 262144 | tf_op jit(solution)/shard_map/all_to_all | solution.py:514
  50.6 62.2 %all-to-all-start.1 = ((bf16[128,64,128]{2,1,0:T(8,128)(2,1)}), bf16[128,64,128]{2,1,0:T(8,128)(2,1)}, u32[]{:S(2)}, u32[]{:S(2)}) async-start(bf16[128,64,128]{2,1,0:T(8,128)(2,1)} %bitcast.16), calls=%async_computation.1 | async-start | bytes 4194304 | tf_op jit(solution)/shard_map/all_to_all | solution.py:519
  116.9 12.2 %collective-permute-start = (bf16[512,128]{1,0:T(8,128)(2,1)}, bf16[512,128]{1,0:T(8,128)(2,1)S(1)}, u32[]{:S(2)}, u32[]{:S(2)}) collective-permute-start(bf16[512,128]{1,0:T(8,128)(2,1)} %spectra_travel.1), channel_id=1, source_target_pairs={{0,127},{1,126},{2,125},{3,124},{4,123},{5,122},{6,121},{7,120},{8... | collective-permute-start | bytes 393224 | tf_op jit(solution)/shard_map/ppermute | solution.py:525

commit v4 on v3

--- a/solution.py
+++ b/solution.py
@@ -19,9 +19,10 @@
 MAP_READS = 2
 SLOTS = 16
 GRAMS = 16
-PARTS = 4
 UNROLL = 4
 VMEM_LIMIT = 67043328
+ALM_VMEM = 10 * 1024 * 1024
+SPECTRA_VMEM = 24 * 1024 * 1024
 VMEM_SPEC = pl.BlockSpec(memory_space=pltpu.VMEM)
 SMEM_SPEC = pl.BlockSpec(memory_space=pltpu.SMEM)
 HBM_SPEC = pl.BlockSpec(memory_space=pltpu.HBM)
@@ -203,12 +204,11 @@
 
 def alm_products(split, legendre_hbm, legendre_ref, operand_ref, held_ref, pad, height, sems):
     degrees = legendre_ref.shape[0]
-    reads = sems.shape[0]
     for tile in range(degrees // height):
         first_row = tile * height
         place = pl.ds(first_row, height)
-        if first_row % (degrees // reads) == 0:
-            legendre_read(legendre_hbm, legendre_ref, sems, first_row * reads // degrees).wait()
+        if sems is not None and first_row % (degrees // sems.shape[0]) == 0:
+            legendre_read(legendre_hbm, legendre_ref, sems, first_row * sems.shape[0] // degrees).wait()
         slot = (first_row >= split).astype(jnp.int32)
         held_ref[pad + first_row : pad + first_row + height] = jnp.dot(
             legendre_ref[place], operand_ref[slot], preferred_element_type=jnp.float32
@@ -298,10 +298,8 @@
 
 
 def alm_kernel(
-    height, plan_ref, given_ref, legendre_hbm, alm_hbm, weight_ref, given32_ref, operand_ref, held_ref, legendre_ref, sems, sem
+    height, plan_ref, given_ref, legendre_ref, alm_hbm, weight_ref, given32_ref, operand_ref, held_ref, sem
 ):
-    for part in range(sems.shape[0]):
-        legendre_read(legendre_hbm, legendre_ref, sems, part).start()
     given32_ref[...] = given_ref[...].astype(jnp.float32)
     make_operands(given32_ref, operand_ref)
     cycles = given_ref.shape[0] // 4
@@ -311,7 +309,7 @@
     pixels = jnp.sum(jnp.where(lane < 3, 0.0, pieces))
     weight_ref[...] = jnp.full(weight_ref.shape, square / pixels, jnp.float32)
     split = legendre_ref.shape[0] - plan_ref[0]
-    alm_products(split, legendre_hbm, legendre_ref, operand_ref, held_ref, 0, height, sems)
+    alm_products(split, None, legendre_ref, operand_ref, held_ref, 0, height, None)
     copy = pltpu.make_async_copy(held_ref, alm_hbm, sem)
     copy.start()
     copy.wait()
@@ -326,47 +324,25 @@
             jax.ShapeDtypeStruct((degrees, columns), jnp.float32),
             jax.ShapeDtypeStruct((1, columns), jnp.float32),
         ),
-        in_specs=[SMEM_SPEC, VMEM_SPEC, HBM_SPEC],
+        in_specs=[SMEM_SPEC, VMEM_SPEC, VMEM_SPEC],
         out_specs=(HBM_SPEC, VMEM_SPEC),
         scratch_shapes=[
             pltpu.VMEM(given.shape, jnp.float32),
             pltpu.VMEM((2, inner, columns), jnp.bfloat16),
             pltpu.VMEM((degrees, columns), jnp.float32),
-            pltpu.VMEM((degrees, inner), jnp.bfloat16),
-            pltpu.SemaphoreType.DMA((READS,)),
             pltpu.SemaphoreType.DMA,
         ],
-        compiler_params=pltpu.CompilerParams(vmem_limit_bytes=VMEM_LIMIT),
+        compiler_params=pltpu.CompilerParams(vmem_limit_bytes=ALM_VMEM),
         name="packed_alm",
     )(plan, given, legendre)
 
 
 def spectra_kernel(
-    travels, degrees, plan_hbm, orders_hbm, order_row_hbm, weight_hbm, rows_hbm, out_ref,
-    rows_ref, first_ref, second_ref, gram_ref, factor_ref, total_ref, sems, out_sem,
-    plan_ref, order_ref, order_row_ref, weight_ref, small_sems,
+    travels, degrees, plan_ref, order_ref, order_row_ref, weight_ref, rows_ref, out_ref,
+    first_ref, second_ref, gram_ref, factor_ref, total_ref, out_sem,
 ):
-    small = [
-        pltpu.make_async_copy(source, target, small_sems.at[index])
-        for index, (source, target) in enumerate(
-            ((plan_hbm, plan_ref), (orders_hbm, order_ref), (order_row_hbm, order_row_ref), (weight_hbm, weight_ref))
-        )
-    ]
-    for copy in small:
-        copy.start()
     pairs = order_row_ref.shape[1]
     half = rows_ref.shape[0] // pairs // 2
-    parts = sems.shape[0]
-    height = rows_ref.shape[0] // parts
-
-    def reading(part):
-        place = pl.ds(part * height, height)
-        return pltpu.make_async_copy(rows_hbm.at[place], rows_ref.at[place], sems.at[part])
-
-    for part in range(parts):
-        reading(part).start()
-    for copy in small:
-        copy.wait()
     first = plan_ref[1]
     upper = plan_ref[2] == 1
     low_wanted = upper if travels else jnp.logical_not(upper)
@@ -398,9 +374,7 @@
         return carry
 
     def place_rows(body):
-        for part in range(parts):
-            reading(part).wait()
-            lax.fori_loop(part * (pairs // parts), (part + 1) * (pairs // parts), body, 0, unroll=UNROLL)
+        lax.fori_loop(0, pairs, body, 0, unroll=UNROLL)
 
     def gram(rows):
         return lax.dot_general(rows, rows, (((0,), (0,)), ((), ())), preferred_element_type=jnp.float32)
@@ -475,23 +449,17 @@
     return pl.pallas_call(
         functools.partial(spectra_kernel, travels, degrees),
         out_shape=out,
-        in_specs=[HBM_SPEC] * 5,
+        in_specs=[SMEM_SPEC] * 2 + [VMEM_SPEC] * 3,
         out_specs=VMEM_SPEC if travels else HBM_SPEC,
         scratch_shapes=[
-            pltpu.VMEM(rows.shape, jnp.bfloat16),
             pltpu.VMEM((2 * half * PITCH, columns), jnp.float32),
             pltpu.VMEM((half * PITCH, columns), jnp.float32),
             pltpu.VMEM((2 * half, 32, columns), jnp.float32),
             pltpu.VMEM((half, columns), jnp.float32),
             pltpu.VMEM((half * 16, columns), jnp.float32),
-            pltpu.SemaphoreType.DMA((PARTS,)),
             pltpu.SemaphoreType.DMA,
-            pltpu.SMEM(plan.shape, jnp.int32),
-            pltpu.SMEM(low_orders.shape, jnp.int32),
-            pltpu.VMEM((1, pairs), jnp.int32),
-            pltpu.VMEM(weight.shape, jnp.float32),
-            pltpu.SemaphoreType.DMA((4,)),
         ],
+        compiler_params=pltpu.CompilerParams(vmem_limit_bytes=SPECTRA_VMEM),
         name="spectra_travel" if travels else "spectra_stay",
     )(plan, low_orders, low_orders[None], weight, rows)
 

time: 130 us -> 128 us (0.985)
  Pallas kernels: 25.4 us -> 21.3 us
  local copies, waits for them, and re-layouts: 0 us -> 2.19 us
    unnamed x0 -> x6, local copies, waits for them, and re-layouts: none -> 2.19 us
    pallas_call x1, Pallas kernels: 6.65 us -> 4.47 us  [packed_alm(): pl.pallas_call(functools.partial(alm_kernel, height), out_shape=(jax.Shap...]
    pallas_call x2, Pallas kernels: 7.83 us -> 5.92 us  [spectra_rows(): pl.pallas_call(functools.partial(spectra_kernel, travels, degrees), out_s...]
  transfers between devices with their start and end apart: 3 -> 3, of which waited for: 3 -> 3; matrix products, arithmetic and copies ran while one was open for 0% -> 0% of each run, Pallas kernels for 9% -> 7%
where the time goes in v4:
time: 128 us
  waiting for transfers between devices  66.3 us (52%)
  starting transfers between devices  35.3 us (28%)
  Pallas kernels  21.3 us (17%)
  local copies, waits for them, and re-layouts  2.19 us (2%)
  between operations  2.03 us (2%)
    all_to_all x1, waiting for transfers between devices, local(): lax.all_to_all(send.reshape(devices, range_rows, columns), BAND_SUB, spli...  46.6 us
    all_to_all x1, starting transfers between devices, local(): lax.all_to_all(outgoing.reshape(devices, 4, columns), BAND_SUB, split_axi...  27.1 us
    all_to_all x1, waiting for transfers between devices, local(): lax.all_to_all(outgoing.reshape(devices, 4, columns), BAND_SUB, split_axi...  10.7 us
    ppermute x1, waiting for transfers between devices, local(): swapped = lax.ppermute(moving, BAND_SUB, route)  8.91 us
    all_to_all x1, starting transfers between devices, local(): lax.all_to_all(send.reshape(devices, range_rows, columns), BAND_SUB, spli...  8.12 us
    pallas_call x2, Pallas kernels, spectra_rows(): pl.pallas_call(functools.partial(spectra_kernel, travels, degrees), out_s...  5.92 us
    pallas_call x1, Pallas kernels, rows_to_send(): pl.pallas_call(functools.partial(send_kernel, height), out_shape=jax.Shap...  5.38 us
    pallas_call x1, Pallas kernels, packed_alm(): pl.pallas_call(functools.partial(alm_kernel, height), out_shape=(jax.Shap...  4.47 us
  transfers between devices with their start and end apart: 3, of which 3 were waited for; matrix products, arithmetic and copies ran while one was open for 0% of the time, Pallas kernels for 7%

profile of v4, /device:TPU:514, one launch (start us, length us, event | category | flops | bytes accessed | tf_op | source)
XLA Modules:
  0.0 127.8 jit_solution(11258578163335252647)
XLA Ops:
  1.9 4.4 %fourier.1 = bf16[512,128]{1,0:T(8,128)(2,1)} custom-call(s32[1]{0:T(128)S(6)} %copy.10.count_ref, s32[1]{0:T(128)S(6)} %copy.11.offset_ref, s32[1,128]{1,0:T(1,128)} %bitcast.18, f32[1,16384]{1,0:T(1,128)} %mask_hbm.1, bf16[64,16384]{1,0:T(8,128)(2,1)} %bitcast.22), custom_call_target="tpu_custom_call" | custom-call | tf_op jit(solution)/shard_map/fourier/pallas_call | solution.py:148
  6.3 27.1 %all-to-all-start = ((bf16[128,4,128]{2,1,0:T(4,128)(2,1)}), bf16[128,4,128]{2,1,0:T(4,128)(2,1)}, u32[]{:S(2)}, u32[]{:S(2)}) async-start(bf16[128,4,128]{2,1,0:T(4,128)(2,1)} %bitcast.23), calls=%async_computation | async-start | bytes 262144 | tf_op jit(solution)/shard_map/all_to_all | solution.py:482
  33.4 1.2 plan.1.plan_ref.plan_hbm
  34.6 10.7 %all-to-all-done = bf16[128,4,128]{2,1,0:T(4,128)(2,1)} async-done(((bf16[128,4,128]{2,1,0:T(4,128)(2,1)}), bf16[128,4,128]{2,1,0:T(4,128)(2,1)}, u32[]{:S(2)}, u32[]{:S(2)}) %all-to-all-start) | async-done | bytes 131104 | tf_op jit(solution)/shard_map/all_to_all | solution.py:482
  45.3 5.4 %rows_to_send.1 = bf16[8192,128]{1,0:T(8,128)(2,1)} custom-call(s32[3]{0:T(128)} %plan.1.plan_ref.plan_hbm, bf16[512,128]{1,0:T(8,128)(2,1)} %bitcast.4.given_ref.given_hbm, bf16[8192,256]{1,0:T(8,128)(2,1)} %bitcast.16), custom_call_target="tpu_custom_call" | custom-call | tf_op jit(solution)/shard_map/rows_to_send/pallas_call | solution.py:278
  50.7 0.0 copy-start.2
  50.7 8.1 %all-to-all-start.1 = ((bf16[128,64,128]{2,1,0:T(8,128)(2,1)}), bf16[128,64,128]{2,1,0:T(8,128)(2,1)S(1)}, u32[]{:S(2)}, u32[]{:S(2)}) async-start(bf16[128,64,128]{2,1,0:T(8,128)(2,1)} %bitcast.21), calls=%async_computation.1 | async-start | bytes 4194304 | tf_op jit(solution)/shard_map/all_to_all | solution.py:487
  58.8 0.0 copy-done.2
  58.8 0.0 copy-start
  58.8 2.2 %copy-done = bf16[1,8192,256]{2,1,0:T(8,128)(2,1)S(1)} copy-done((bf16[1,8192,256]{2,1,0:T(8,128)(2,1)S(1)}, bf16[1,8192,256]{2,1,0:T(8,128)(2,1)}, u32[]{:S(2)}) %copy-start) | copy-done | bytes 4194328
  61.0 0.0 copy-start.1
  61.0 4.5 %packed_alm.1 = (f32[8192,128]{1,0:T(8,128)}, f32[1,128]{1,0:T(1,128)S(1)}) custom-call(s32[3]{0:T(128)S(1)} %copy-done.2, bf16[512,128]{1,0:T(8,128)(2,1)} %bitcast.4.given_ref.given_hbm, bf16[8192,256]{1,0:T(8,128)(2,1)S(1)} %bitcast.17), custom_call_target="tpu_custom_call" | custom-call | tf_op jit(solution)/shard_map/packed_alm/pallas_call | solution.py:321
  65.5 46.6 %all-to-all-done.1 = bf16[128,64,128]{2,1,0:T(8,128)(2,1)S(1)} async-done(((bf16[128,64,128]{2,1,0:T(8,128)(2,1)}), bf16[128,64,128]{2,1,0:T(8,128)(2,1)S(1)}, u32[]{:S(2)}, u32[]{:S(2)}) %all-to-all-start.1) | async-done | bytes 2097184 | tf_op jit(solution)/shard_map/all_to_all | solution.py:487
  112.1 0.0 copy-done.1
  112.1 3.0 %spectra_travel.1 = bf16[512,128]{1,0:T(8,128)(2,1)S(1)} custom-call(s32[3]{0:T(128)S(1)} %copy-done.2, s32[128]{0:T(128)S(1)} %copy-done.1, s32[1,128]{1,0:T(1,128)S(1)} %bitcast.19, f32[1,128]{1,0:T(1,128)S(1)} %get-tuple-element.5.weight_ref, bf16[8192,128]{1,0:T(8,128)(2,1)S(1)} %bitcast.14), custom_call_target="tpu_custom_call" | custom-call | tf_op jit(solution)/shard_map/spectra_travel/pallas_call | solution.py:449
  115.1 0.1 collective-permute-start
  115.2 3.0 %spectra_stay.1 = f32[1024,128]{1,0:T(8,128)} custom-call(s32[3]{0:T(128)S(1)} %copy-done.2, s32[128]{0:T(128)S(1)} %copy-done.1, s32[1,128]{1,0:T(1,128)S(1)} %bitcast.20, f32[1,128]{1,0:T(1,128)S(1)} %get-tuple-element.5.weight_ref, bf16[8192,128]{1,0:T(8,128)(2,1)S(1)} %bitcast.15), custom_call_target="tpu_custom_call" | custom-call | tf_op jit(solution)/shard_map/spectra_stay/pallas_call | solution.py:449
  118.2 8.9 %collective-permute-done = bf16[512,128]{1,0:T(8,128)(2,1)S(1)} collective-permute-done((bf16[512,128]{1,0:T(8,128)(2,1)S(1)}, bf16[512,128]{1,0:T(8,128)(2,1)S(1)}, u32[]{:S(2)}, u32[]{:S(2)}) %collective-permute-start) | collective-permute-done | bytes 131104 | tf_op jit(solution)/shard_map/ppermute | solution.py:493
  127.1 0.7 convert_dynamic-update-slice_fusion
Async XLA Ops:
  6.3 39.0 %all-to-all-start = ((bf16[128,4,128]{2,1,0:T(4,128)(2,1)}), bf16[128,4,128]{2,1,0:T(4,128)(2,1)}, u32[]{:S(2)}, u32[]{:S(2)}) async-start(bf16[128,4,128]{2,1,0:T(4,128)(2,1)} %bitcast.23), calls=%async_computation | async-start | bytes 262144 | tf_op jit(solution)/shard_map/all_to_all | solution.py:482
  50.7 8.1 %copy-start.2 = (s32[3]{0:T(128)S(1)}, s32[3]{0:T(128)}, u32[]{:S(2)}) copy-start(s32[3]{0:T(128)} %plan.1.plan_ref.plan_hbm) | copy-start | bytes 40
  50.7 61.4 %all-to-all-start.1 = ((bf16[128,64,128]{2,1,0:T(8,128)(2,1)}), bf16[128,64,128]{2,1,0:T(8,128)(2,1)S(1)}, u32[]{:S(2)}, u32[]{:S(2)}) async-start(bf16[128,64,128]{2,1,0:T(8,128)(2,1)} %bitcast.21), calls=%async_computation.1 | async-start | bytes 4194304 | tf_op jit(solution)/shard_map/all_to_all | solution.py:487
  58.8 2.2 %copy-start = (bf16[1,8192,256]{2,1,0:T(8,128)(2,1)S(1)}, bf16[1,8192,256]{2,1,0:T(8,128)(2,1)}, u32[]{:S(2)}) copy-start(bf16[1,8192,256]{2,1,0:T(8,128)(2,1)} %param.11) | copy-start | bytes 12582916
  61.0 51.1 %copy-start.1 = (s32[128]{0:T(128)S(1)}, s32[128]{0:T(128)}, u32[]{:S(2)}) copy-start(s32[128]{0:T(128)} %order_ref.3) | copy-start | bytes 1540
  115.1 12.0 %collective-permute-start = (bf16[512,128]{1,0:T(8,128)(2,1)S(1)}, bf16[512,128]{1,0:T(8,128)(2,1)S(1)}, u32[]{:S(2)}, u32[]{:S(2)}) collective-permute-start(bf16[512,128]{1,0:T(8,128)(2,1)S(1)} %spectra_travel.1), channel_id=1, source_target_pairs={{0,127},{1,126},{2,125},{3,124},{4,123},{5,122},{6,121},{7,120},{8... | collective-permute-start | bytes 393224 | tf_op jit(solution)/shard_map/ppermute | solution.py:493

commit v5 on v4

--- a/solution.py
+++ b/solution.py
@@ -18,9 +18,10 @@
 PIECES = 2
 MAP_READS = 2
 SLOTS = 16
-GRAMS = 16
-UNROLL = 4
-VMEM_LIMIT = 67043328
+GRAMS = 32
+UNROLL = 8
+PLAN_VMEM = 8 * 1024 * 1024
+SEND_VMEM = 52 * 1024 * 1024
 ALM_VMEM = 10 * 1024 * 1024
 SPECTRA_VMEM = 24 * 1024 * 1024
 VMEM_SPEC = pl.BlockSpec(memory_space=pltpu.VMEM)
@@ -180,7 +181,7 @@
         out_shape=jax.ShapeDtypeStruct((3,), jnp.int32),
         in_specs=[SMEM_SPEC, SMEM_SPEC],
         out_specs=SMEM_SPEC,
-        compiler_params=pltpu.CompilerParams(vmem_limit_bytes=VMEM_LIMIT),
+        compiler_params=pltpu.CompilerParams(vmem_limit_bytes=PLAN_VMEM),
         name="plan",
     )(device, low_orders)
 
@@ -227,20 +228,14 @@
 
 
 def send_kernel(
-    height, plan_hbm, given_hbm, legendre_hbm, send_hbm,
-    given_ref, given32_ref, operand_ref, held_ref, legendre_ref, send_ref, sems, send_sems, given_sem, plan_ref, plan_sem,
+    height, plan_ref, given_ref, legendre_hbm, send_hbm,
+    given32_ref, operand_ref, held_ref, legendre_ref, send_ref, sems, send_sems,
 ):
-    plan_read = pltpu.make_async_copy(plan_hbm, plan_ref, plan_sem)
-    plan_read.start()
-    given_read = pltpu.make_async_copy(given_hbm, given_ref, given_sem)
-    given_read.start()
     for part in range(sems.shape[0]):
         legendre_read(legendre_hbm, legendre_ref, sems, part).start()
     cycles = given_ref.shape[0] // 4
     degrees = legendre_ref.shape[0]
-    plan_read.wait()
     order = plan_ref[0]
-    given_read.wait()
     given32_ref[...] = given_ref[...].astype(jnp.float32)
     make_operands(given32_ref, operand_ref)
     alm_products(degrees - order, legendre_hbm, legendre_ref, operand_ref, held_ref, 32, height, sems)
@@ -278,10 +273,9 @@
     return pl.pallas_call(
         functools.partial(send_kernel, height),
         out_shape=jax.ShapeDtypeStruct((degrees, columns), jnp.bfloat16),
-        in_specs=[HBM_SPEC] * 3,
+        in_specs=[SMEM_SPEC, VMEM_SPEC, HBM_SPEC],
         out_specs=HBM_SPEC,
         scratch_shapes=[
-            pltpu.VMEM(given.shape, jnp.bfloat16),
             pltpu.VMEM(given.shape, jnp.float32),
             pltpu.VMEM((2, inner, columns), jnp.bfloat16),
             pltpu.VMEM((degrees + 64, columns), jnp.float32),
@@ -289,10 +283,8 @@
             pltpu.VMEM((degrees, columns), jnp.bfloat16),
             pltpu.SemaphoreType.DMA((READS,)),
             pltpu.SemaphoreType.DMA((PIECES,)),
-            pltpu.SemaphoreType.DMA,
-            pltpu.SMEM(plan.shape, jnp.int32),
-            pltpu.SemaphoreType.DMA,
         ],
+        compiler_params=pltpu.CompilerParams(vmem_limit_bytes=SEND_VMEM),
         name="rows_to_send",
     )(plan, given, legendre)
 

time: 128 us -> 128 us (level)
  transfers between devices with their start and end apart: 3 -> 3, of which waited for: 3 -> 3; matrix products, arithmetic and copies ran while one was open for 0% -> 0% of each run, Pallas kernels for 7% -> 6%
where the time goes in v5:
time: 128 us; the launch traced here: 127 us
  waiting for transfers between devices  66.8 us (52%)
  starting transfers between devices  34.7 us (27%)
  Pallas kernels  20.8 us (16%)
  local copies, waits for them, and re-layouts  2.19 us (2%)
  between operations  2.04 us (2%)
    all_to_all x1, waiting for transfers between devices, local(): lax.all_to_all(send.reshape(devices, range_rows, columns), BAND_SUB, spli...  47 us
    all_to_all x1, starting transfers between devices, local(): lax.all_to_all(outgoing.reshape(devices, 4, columns), BAND_SUB, split_axi...  26.4 us
    all_to_all x1, waiting for transfers between devices, local(): lax.all_to_all(outgoing.reshape(devices, 4, columns), BAND_SUB, split_axi...  10.6 us
    ppermute x1, waiting for transfers between devices, local(): swapped = lax.ppermute(moving, BAND_SUB, route)  9.12 us
    all_to_all x1, starting transfers between devices, local(): lax.all_to_all(send.reshape(devices, range_rows, columns), BAND_SUB, spli...  8.12 us
    pallas_call x1, Pallas kernels, rows_to_send(): pl.pallas_call(functools.partial(send_kernel, height), out_shape=jax.Shap...  5.77 us
    pallas_call x2, Pallas kernels, spectra_rows(): pl.pallas_call(functools.partial(spectra_kernel, travels, degrees), out_s...  5.44 us
    pallas_call x1, Pallas kernels, fourier(): pl.pallas_call(functools.partial(fourier_kernel, degrees), out_shape=jax....  4.35 us
  transfers between devices with their start and end apart: 3, of which 3 were waited for; matrix products, arithmetic and copies ran while one was open for 0% of the time, Pallas kernels for 6%

profile of v5, /device:TPU:514, one launch (start us, length us, event | category | flops | bytes accessed | tf_op | source)
XLA Modules:
  0.0 127.2 jit_solution(10537874005961280656)
XLA Ops:
  0.6 0.0 copy-start.1
  1.9 4.4 %fourier.1 = bf16[512,128]{1,0:T(8,128)(2,1)} custom-call(s32[1]{0:T(128)S(6)} %copy.10.count_ref, s32[1]{0:T(128)S(6)} %copy.11.offset_ref, s32[1,128]{1,0:T(1,128)} %bitcast.20, f32[1,16384]{1,0:T(1,128)} %mask_hbm.1, bf16[64,16384]{1,0:T(8,128)(2,1)} %bitcast.24), custom_call_target="tpu_custom_call" | custom-call | tf_op jit(solution)/shard_map/fourier/pallas_call | solution.py:149
  6.3 26.4 %all-to-all-start = ((bf16[128,4,128]{2,1,0:T(4,128)(2,1)}), bf16[128,4,128]{2,1,0:T(4,128)(2,1)S(1)}, u32[]{:S(2)}, u32[]{:S(2)}) async-start(bf16[128,4,128]{2,1,0:T(4,128)(2,1)} %bitcast.25), calls=%async_computation | async-start | bytes 262144 | tf_op jit(solution)/shard_map/all_to_all | solution.py:474
  32.8 0.0 copy-done.1
  32.8 1.1 plan.1.plan_ref
  33.9 10.6 %all-to-all-done = bf16[128,4,128]{2,1,0:T(4,128)(2,1)S(1)} async-done(((bf16[128,4,128]{2,1,0:T(4,128)(2,1)}), bf16[128,4,128]{2,1,0:T(4,128)(2,1)S(1)}, u32[]{:S(2)}, u32[]{:S(2)}) %all-to-all-start) | async-done | bytes 131104 | tf_op jit(solution)/shard_map/all_to_all | solution.py:474
  44.5 5.8 %rows_to_send.1 = bf16[8192,128]{1,0:T(8,128)(2,1)} custom-call(s32[3]{0:T(128)S(1)} %plan.1.plan_ref, bf16[512,128]{1,0:T(8,128)(2,1)S(1)} %bitcast.18, bf16[8192,256]{1,0:T(8,128)(2,1)} %bitcast.16), custom_call_target="tpu_custom_call" | custom-call | tf_op jit(solution)/shard_map/rows_to_send/pallas_call | solution.py:273
  50.3 8.1 %all-to-all-start.1 = ((bf16[128,64,128]{2,1,0:T(8,128)(2,1)}), bf16[128,64,128]{2,1,0:T(8,128)(2,1)S(1)}, u32[]{:S(2)}, u32[]{:S(2)}) async-start(bf16[128,64,128]{2,1,0:T(8,128)(2,1)} %bitcast.23), calls=%async_computation.1 | async-start | bytes 4194304 | tf_op jit(solution)/shard_map/all_to_all | solution.py:479
  58.4 0.0 copy-start
  58.5 2.2 %copy-done = bf16[1,8192,256]{2,1,0:T(8,128)(2,1)S(1)} copy-done((bf16[1,8192,256]{2,1,0:T(8,128)(2,1)S(1)}, bf16[1,8192,256]{2,1,0:T(8,128)(2,1)}, u32[]{:S(2)}) %copy-start) | copy-done | bytes 4194328
  60.6 4.1 %packed_alm.1 = (f32[8192,128]{1,0:T(8,128)}, f32[1,128]{1,0:T(1,128)S(1)}) custom-call(s32[3]{0:T(128)S(1)} %plan.1.plan_ref, bf16[512,128]{1,0:T(8,128)(2,1)S(1)} %bitcast.19, bf16[8192,256]{1,0:T(8,128)(2,1)S(1)} %bitcast.17), custom_call_target="tpu_custom_call" | custom-call | tf_op jit(solution)/shard_map/packed_alm/pallas_call | solution.py:313
  64.7 47.0 %all-to-all-done.1 = bf16[128,64,128]{2,1,0:T(8,128)(2,1)S(1)} async-done(((bf16[128,64,128]{2,1,0:T(8,128)(2,1)}), bf16[128,64,128]{2,1,0:T(8,128)(2,1)S(1)}, u32[]{:S(2)}, u32[]{:S(2)}) %all-to-all-start.1) | async-done | bytes 2097184 | tf_op jit(solution)/shard_map/all_to_all | solution.py:479
  111.8 2.7 %spectra_travel.1 = bf16[512,128]{1,0:T(8,128)(2,1)S(1)} custom-call(s32[3]{0:T(128)S(1)} %plan.1.plan_ref, s32[128]{0:T(128)S(1)} %copy-done.1, s32[1,128]{1,0:T(1,128)S(1)} %bitcast.21, f32[1,128]{1,0:T(1,128)S(1)} %get-tuple-element.5.weight_ref, bf16[8192,128]{1,0:T(8,128)(2,1)S(1)} %bitcast.14), custom_call_target="tpu_custom_call" | custom-call | tf_op jit(solution)/shard_map/spectra_travel/pallas_call | solution.py:441
  114.5 0.1 collective-permute-start
  114.6 2.7 %spectra_stay.1 = f32[1024,128]{1,0:T(8,128)} custom-call(s32[3]{0:T(128)S(1)} %plan.1.plan_ref, s32[128]{0:T(128)S(1)} %copy-done.1, s32[1,128]{1,0:T(1,128)S(1)} %bitcast.22, f32[1,128]{1,0:T(1,128)S(1)} %get-tuple-element.5.weight_ref, bf16[8192,128]{1,0:T(8,128)(2,1)S(1)} %bitcast.15), custom_call_target="tpu_custom_call" | custom-call | tf_op jit(solution)/shard_map/spectra_stay/pallas_call | solution.py:441
  117.4 9.1 %collective-permute-done = bf16[512,128]{1,0:T(8,128)(2,1)S(1)} collective-permute-done((bf16[512,128]{1,0:T(8,128)(2,1)S(1)}, bf16[512,128]{1,0:T(8,128)(2,1)S(1)}, u32[]{:S(2)}, u32[]{:S(2)}) %collective-permute-start) | collective-permute-done | bytes 131104 | tf_op jit(solution)/shard_map/ppermute | solution.py:485
  126.5 0.7 convert_dynamic-update-slice_fusion
Async XLA Ops:
  0.6 32.1 %copy-start.1 = (s32[128]{0:T(128)S(1)}, s32[128]{0:T(128)}, u32[]{:S(2)}) copy-start(s32[128]{0:T(128)} %order_ref.3) | copy-start | bytes 1540
  6.3 38.2 %all-to-all-start = ((bf16[128,4,128]{2,1,0:T(4,128)(2,1)}), bf16[128,4,128]{2,1,0:T(4,128)(2,1)S(1)}, u32[]{:S(2)}, u32[]{:S(2)}) async-start(bf16[128,4,128]{2,1,0:T(4,128)(2,1)} %bitcast.25), calls=%async_computation | async-start | bytes 262144 | tf_op jit(solution)/shard_map/all_to_all | solution.py:474
  50.3 61.5 %all-to-all-start.1 = ((bf16[128,64,128]{2,1,0:T(8,128)(2,1)}), bf16[128,64,128]{2,1,0:T(8,128)(2,1)S(1)}, u32[]{:S(2)}, u32[]{:S(2)}) async-start(bf16[128,64,128]{2,1,0:T(8,128)(2,1)} %bitcast.23), calls=%async_computation.1 | async-start | bytes 4194304 | tf_op jit(solution)/shard_map/all_to_all | solution.py:479
  58.4 2.2 %copy-start = (bf16[1,8192,256]{2,1,0:T(8,128)(2,1)S(1)}, bf16[1,8192,256]{2,1,0:T(8,128)(2,1)}, u32[]{:S(2)}) copy-start(bf16[1,8192,256]{2,1,0:T(8,128)(2,1)} %param.11) | copy-start | bytes 12582916
  114.5 12.0 %collective-permute-start = (bf16[512,128]{1,0:T(8,128)(2,1)S(1)}, bf16[512,128]{1,0:T(8,128)(2,1)S(1)}, u32[]{:S(2)}, u32[]{:S(2)}) collective-permute-start(bf16[512,128]{1,0:T(8,128)(2,1)S(1)} %spectra_travel.1), channel_id=1, source_target_pairs={{0,127},{1,126},{2,125},{3,124},{4,123},{5,122},{6,121},{7,120},{8... | collective-permute-start | bytes 393224 | tf_op jit(solution)/shard_map/ppermute | solution.py:485

commit v6 on v5

--- a/solution.py
+++ b/solution.py
@@ -16,11 +16,11 @@
 PITCH = 132
 READS = 2
 PIECES = 2
+DEVICES = 4
 MAP_READS = 2
 SLOTS = 16
 GRAMS = 32
 UNROLL = 8
-PLAN_VMEM = 8 * 1024 * 1024
 SEND_VMEM = 52 * 1024 * 1024
 ALM_VMEM = 10 * 1024 * 1024
 SPECTRA_VMEM = 24 * 1024 * 1024
@@ -166,26 +166,6 @@
     )(count, offset, low_orders, mask, maps)
 
 
-def plan_kernel(range_rows, device_ref, orders_ref, plan_ref):
-    device = device_ref[0]
-    devices = orders_ref.shape[0]
-    upper = (device >= devices // 2).astype(jnp.int32)
-    plan_ref[0] = orders_ref[device]
-    plan_ref[1] = jnp.minimum(device, devices - 1 - device) * range_rows + upper * (range_rows // 2)
-    plan_ref[2] = upper
-
-
-def plan_of(device, low_orders, range_rows):
-    return pl.pallas_call(
-        functools.partial(plan_kernel, range_rows),
-        out_shape=jax.ShapeDtypeStruct((3,), jnp.int32),
-        in_specs=[SMEM_SPEC, SMEM_SPEC],
-        out_specs=SMEM_SPEC,
-        compiler_params=pltpu.CompilerParams(vmem_limit_bytes=PLAN_VMEM),
-        name="plan",
-    )(device, low_orders)
-
-
 def make_operands(given32_ref, operand_ref):
     columns = given32_ref.shape[1]
     cycles = given32_ref.shape[0] // 4
@@ -228,14 +208,14 @@
 
 
 def send_kernel(
-    height, plan_ref, given_ref, legendre_hbm, send_hbm,
+    height, order_ref, given_ref, legendre_hbm, send_hbm,
     given32_ref, operand_ref, held_ref, legendre_ref, send_ref, sems, send_sems,
 ):
     for part in range(sems.shape[0]):
         legendre_read(legendre_hbm, legendre_ref, sems, part).start()
     cycles = given_ref.shape[0] // 4
     degrees = legendre_ref.shape[0]
-    order = plan_ref[0]
+    order = order_ref[0]
     given32_ref[...] = given_ref[...].astype(jnp.float32)
     make_operands(given32_ref, operand_ref)
     alm_products(degrees - order, legendre_hbm, legendre_ref, operand_ref, held_ref, 32, height, sems)
@@ -259,7 +239,7 @@
             send_ref[pl.ds(start + half, half)] = mirror.astype(jnp.bfloat16)
             return carry
 
-        lax.fori_loop(0, batch, one, 0, unroll=4)
+        lax.fori_loop(0, batch, one, 0, unroll=DEVICES)
         place = pl.ds(piece * batch * 2 * half, batch * 2 * half)
         pltpu.make_async_copy(send_ref.at[place], send_hbm.at[place], send_sems.at[piece]).start()
     for piece in range(send_sems.shape[0]):
@@ -267,7 +247,7 @@
         pltpu.make_async_copy(send_ref.at[place], send_hbm.at[place], send_sems.at[piece]).wait()
 
 
-def rows_to_send(plan, given, legendre, height=512):
+def rows_to_send(order, given, legendre, height=512):
     degrees, inner = legendre.shape
     columns = given.shape[1]
     return pl.pallas_call(
@@ -286,11 +266,11 @@
         ],
         compiler_params=pltpu.CompilerParams(vmem_limit_bytes=SEND_VMEM),
         name="rows_to_send",
-    )(plan, given, legendre)
+    )(order, given, legendre)
 
 
 def alm_kernel(
-    height, plan_ref, given_ref, legendre_ref, alm_hbm, weight_ref, given32_ref, operand_ref, held_ref, sem
+    height, order_ref, given_ref, legendre_ref, alm_hbm, weight_ref, given32_ref, operand_ref, held_ref, sem
 ):
     given32_ref[...] = given_ref[...].astype(jnp.float32)
     make_operands(given32_ref, operand_ref)
@@ -300,14 +280,14 @@
     square = jnp.sum(jnp.where(lane < 3, pieces, 0.0))
     pixels = jnp.sum(jnp.where(lane < 3, 0.0, pieces))
     weight_ref[...] = jnp.full(weight_ref.shape, square / pixels, jnp.float32)
-    split = legendre_ref.shape[0] - plan_ref[0]
+    split = legendre_ref.shape[0] - order_ref[0]
     alm_products(split, None, legendre_ref, operand_ref, held_ref, 0, height, None)
     copy = pltpu.make_async_copy(held_ref, alm_hbm, sem)
     copy.start()
     copy.wait()
 
 
-def packed_alm(plan, given, legendre, height=512):
+def packed_alm(order, given, legendre, height=512):
     degrees, inner = legendre.shape
     columns = given.shape[1]
     return pl.pallas_call(
@@ -326,17 +306,17 @@
         ],
         compiler_params=pltpu.CompilerParams(vmem_limit_bytes=ALM_VMEM),
         name="packed_alm",
-    )(plan, given, legendre)
+    )(order, given, legendre)
 
 
 def spectra_kernel(
-    travels, degrees, plan_ref, order_ref, order_row_ref, weight_ref, rows_ref, out_ref,
+    travels, degrees, start_ref, upper_ref, order_ref, order_row_ref, weight_ref, rows_ref, out_ref,
     first_ref, second_ref, gram_ref, factor_ref, total_ref, out_sem,
 ):
     pairs = order_row_ref.shape[1]
     half = rows_ref.shape[0] // pairs // 2
-    first = plan_ref[1]
-    upper = plan_ref[2] == 1
+    first = start_ref[0]
+    upper = upper_ref[0] == 1
     low_wanted = upper if travels else jnp.logical_not(upper)
     step = lax.broadcasted_iota(jnp.int32, (half, 1), 0)
     columns = rows_ref.shape[1]
@@ -433,7 +413,7 @@
         copy.wait()
 
 
-def spectra_rows(plan, low_orders, weight, rows, travels, degrees):
+def spectra_rows(start, upper, low_orders, weight, rows, travels, degrees):
     pairs = low_orders.shape[0]
     columns = rows.shape[1]
     half = rows.shape[0] // pairs // 2
@@ -441,7 +421,7 @@
     return pl.pallas_call(
         functools.partial(spectra_kernel, travels, degrees),
         out_shape=out,
-        in_specs=[SMEM_SPEC] * 2 + [VMEM_SPEC] * 3,
+        in_specs=[SMEM_SPEC] * 3 + [VMEM_SPEC] * 3,
         out_specs=VMEM_SPEC if travels else HBM_SPEC,
         scratch_shapes=[
             pltpu.VMEM((2 * half * PITCH, columns), jnp.float32),
@@ -453,7 +433,7 @@
         ],
         compiler_params=pltpu.CompilerParams(vmem_limit_bytes=SPECTRA_VMEM),
         name="spectra_travel" if travels else "spectra_stay",
-    )(plan, low_orders, low_orders[None], weight, rows)
+    )(start, upper, low_orders, low_orders[None], weight, rows)
 
 
 def in_degree_order(rows, columns):
@@ -474,16 +454,18 @@
     received = lax.all_to_all(
         outgoing.reshape(devices, 4, columns), BAND_SUB, split_axis=0, concat_axis=0, tiled=True
     ).reshape(4 * devices, columns)
-    plan = plan_of(device_index[None], low_orders, range_rows)
-    send = rows_to_send(plan, received, legendre[0])
+    order = lax.dynamic_slice_in_dim(low_orders, device_index, 1, 0)
+    send = rows_to_send(order, received, legendre[0])
     incoming = lax.all_to_all(
         send.reshape(devices, range_rows, columns), BAND_SUB, split_axis=0, concat_axis=0, tiled=True
     ).reshape(-1, columns)
-    alm, weight = packed_alm(plan, received, legendre[0])
+    alm, weight = packed_alm(order, received, legendre[0])
+    upper = (device_index >= devices // 2).astype(jnp.int32)
+    start = jnp.minimum(device_index, devices - 1 - device_index) * range_rows + upper * (range_rows // 2)
     route = [(device, devices - 1 - device) for device in range(devices)]
-    moving = spectra_rows(plan, low_orders, weight, incoming, True, degree_count)
+    moving = spectra_rows(start[None], upper[None], low_orders, weight, incoming, True, degree_count)
     swapped = lax.ppermute(moving, BAND_SUB, route)
-    kept = spectra_rows(plan, low_orders, weight, incoming, False, degree_count)
+    kept = spectra_rows(start[None], upper[None], low_orders, weight, incoming, False, degree_count)
     spectra = lax.dynamic_update_slice_in_dim(kept, swapped.astype(jnp.float32), swapped.shape[0], 0)
     return (alm[None], in_degree_order(spectra, columns))
 

time: 128 us -> 128 us (level)
  transfers between devices with their start and end apart: 3 -> 3, of which waited for: 3 -> 3; matrix products, arithmetic and copies ran while one was open for 0% -> 1% of each run, Pallas kernels for 6% -> 5%
where the time goes in v6:
time: 128 us; the launch traced here: 127 us
  waiting for transfers between devices  67.1 us (52%)
  starting transfers between devices  34.7 us (27%)
  Pallas kernels  20 us (16%)
  local copies, waits for them, and re-layouts  2.84 us (2%)
  between operations  2.04 us (2%)
    all_to_all x1, waiting for transfers between devices, local(): lax.all_to_all(send.reshape(devices, range_rows, columns), BAND_SUB, spli...  46.9 us
    all_to_all x1, starting transfers between devices, local(): lax.all_to_all(outgoing.reshape(devices, 4, columns), BAND_SUB, split_axi...  26.4 us
    all_to_all x1, waiting for transfers between devices, local(): lax.all_to_all(outgoing.reshape(devices, 4, columns), BAND_SUB, split_axi...  11.1 us
    ppermute x1, waiting for transfers between devices, local(): swapped = lax.ppermute(moving, BAND_SUB, route)  9.13 us
    all_to_all x1, starting transfers between devices, local(): lax.all_to_all(send.reshape(devices, range_rows, columns), BAND_SUB, spli...  8.12 us
    pallas_call x1, Pallas kernels, rows_to_send(): pl.pallas_call(functools.partial(send_kernel, height), out_shape=jax.Shap...  5.95 us
    pallas_call x2, Pallas kernels, spectra_rows(): pl.pallas_call(functools.partial(spectra_kernel, travels, degrees), out_s...  5.43 us
    pallas_call x1, Pallas kernels, fourier(): pl.pallas_call(functools.partial(fourier_kernel, degrees), out_shape=jax....  4.35 us
  transfers between devices with their start and end apart: 3, of which 3 were waited for; matrix products, arithmetic and copies ran while one was open for 1% of the time, Pallas kernels for 5%

profile of v6, /device:TPU:514, one launch (start us, length us, event | category | flops | bytes accessed | tf_op | source)
XLA Modules:
  0.0 127.4 jit_solution(18210948006468597940)
XLA Ops:
  0.6 0.0 copy-start.1
  1.9 4.4 %fourier.1 = bf16[512,128]{1,0:T(8,128)(2,1)} custom-call(s32[1]{0:T(128)S(6)} %copy.10.count_ref, s32[1]{0:T(128)S(6)} %copy.11.offset_ref, s32[1,128]{1,0:T(1,128)} %bitcast.21, f32[1,16384]{1,0:T(1,128)} %mask_hbm.1, bf16[64,16384]{1,0:T(8,128)(2,1)} %bitcast.25), custom_call_target="tpu_custom_call" | custom-call | tf_op jit(solution)/shard_map/fourier/pallas_call | solution.py:149
  6.3 26.4 %all-to-all-start = ((bf16[128,4,128]{2,1,0:T(4,128)(2,1)}), bf16[128,4,128]{2,1,0:T(4,128)(2,1)S(1)}, u32[]{:S(2)}, u32[]{:S(2)}) async-start(bf16[128,4,128]{2,1,0:T(4,128)(2,1)} %bitcast.27), calls=%async_computation | async-start | bytes 262144 | tf_op jit(solution)/shard_map/all_to_all | solution.py:454
  32.8 0.0 copy-done.1
  32.8 0.7 dynamic_slice.3.order_ref
  33.4 11.1 %all-to-all-done = bf16[128,4,128]{2,1,0:T(4,128)(2,1)S(1)} async-done(((bf16[128,4,128]{2,1,0:T(4,128)(2,1)}), bf16[128,4,128]{2,1,0:T(4,128)(2,1)S(1)}, u32[]{:S(2)}, u32[]{:S(2)}) %all-to-all-start) | async-done | bytes 131104 | tf_op jit(solution)/shard_map/all_to_all | solution.py:454
  44.5 6.0 %rows_to_send.1 = bf16[8192,128]{1,0:T(8,128)(2,1)} custom-call(s32[1]{0:T(128)} %dynamic_slice.3.order_ref, bf16[512,128]{1,0:T(8,128)(2,1)S(1)} %bitcast.19, bf16[8192,256]{1,0:T(8,128)(2,1)} %bitcast.17), custom_call_target="tpu_custom_call" | custom-call | tf_op jit(solution)/shard_map/rows_to_send/pallas_call | solution.py:253
  50.5 8.1 %all-to-all-start.1 = ((bf16[128,64,128]{2,1,0:T(8,128)(2,1)}), bf16[128,64,128]{2,1,0:T(8,128)(2,1)S(1)}, u32[]{:S(2)}, u32[]{:S(2)}) async-start(bf16[128,64,128]{2,1,0:T(8,128)(2,1)} %bitcast.24), calls=%async_computation.1 | async-start | bytes 4194304 | tf_op jit(solution)/shard_map/all_to_all | solution.py:459
  58.6 0.0 copy-start
  58.6 2.2 %copy-done = bf16[1,8192,256]{2,1,0:T(8,128)(2,1)S(1)} copy-done((bf16[1,8192,256]{2,1,0:T(8,128)(2,1)S(1)}, bf16[1,8192,256]{2,1,0:T(8,128)(2,1)}, u32[]{:S(2)}) %copy-start) | copy-done | bytes 4194328
  60.8 4.2 %packed_alm.1 = (f32[8192,128]{1,0:T(8,128)}, f32[1,128]{1,0:T(1,128)S(1)}) custom-call(s32[1]{0:T(128)} %dynamic_slice.3.order_ref, bf16[512,128]{1,0:T(8,128)(2,1)S(1)} %bitcast.20, bf16[8192,256]{1,0:T(8,128)(2,1)S(1)} %bitcast.18), custom_call_target="tpu_custom_call" | custom-call | tf_op jit(solution)/shard_map/packed_alm/pallas_call | solution.py:293
  65.1 46.9 %all-to-all-done.1 = bf16[128,64,128]{2,1,0:T(8,128)(2,1)S(1)} async-done(((bf16[128,64,128]{2,1,0:T(8,128)(2,1)}), bf16[128,64,128]{2,1,0:T(8,128)(2,1)S(1)}, u32[]{:S(2)}, u32[]{:S(2)}) %all-to-all-start.1) | async-done | bytes 2097184 | tf_op jit(solution)/shard_map/all_to_all | solution.py:459
  111.9 2.7 %spectra_travel.1 = bf16[512,128]{1,0:T(8,128)(2,1)S(1)} custom-call(s32[1]{0:T(128)} %bitcast.6.start_ref, s32[1]{0:T(128)} %bitcast.7.upper_ref, s32[128]{0:T(128)S(1)} %copy-done.1, s32[1,128]{1,0:T(1,128)S(1)} %bitcast.22, f32[1,128]{1,0:T(1,128)S(1)} %get-tuple-element.5.weight_ref, bf16[8192,128]{1,0:T(8,128)(2,1)S(1)} %bitcast.15), custom_call_target="tpu_custom_call" | custom-call | tf_op jit(solution)/shard_map/spectra_travel/pallas_call | solution.py:421
  114.6 0.1 collective-permute-start
  114.8 2.7 %spectra_stay.1 = f32[1024,128]{1,0:T(8,128)} custom-call(s32[1]{0:T(128)} %bitcast.6.start_ref, s32[1]{0:T(128)} %bitcast.7.upper_ref, s32[128]{0:T(128)S(1)} %copy-done.1, s32[1,128]{1,0:T(1,128)S(1)} %bitcast.23, f32[1,128]{1,0:T(1,128)S(1)} %get-tuple-element.5.weight_ref, bf16[8192,128]{1,0:T(8,128)(2,1)S(1)} %bitcast.16), custom_call_target="tpu_custom_call" | custom-call | tf_op jit(solution)/shard_map/spectra_stay/pallas_call | solution.py:421
  117.5 9.1 %collective-permute-done = bf16[512,128]{1,0:T(8,128)(2,1)S(1)} collective-permute-done((bf16[512,128]{1,0:T(8,128)(2,1)S(1)}, bf16[512,128]{1,0:T(8,128)(2,1)S(1)}, u32[]{:S(2)}, u32[]{:S(2)}) %collective-permute-start) | collective-permute-done | bytes 131104 | tf_op jit(solution)/shard_map/ppermute | solution.py:467
  126.7 0.7 convert_dynamic-update-slice_fusion
Async XLA Ops:
  0.6 32.1 %copy-start.1 = (s32[128]{0:T(128)S(1)}, s32[128]{0:T(128)}, u32[]{:S(2)}) copy-start(s32[128]{0:T(128)} %order_ref.3) | copy-start | bytes 1540
  6.3 38.2 %all-to-all-start = ((bf16[128,4,128]{2,1,0:T(4,128)(2,1)}), bf16[128,4,128]{2,1,0:T(4,128)(2,1)S(1)}, u32[]{:S(2)}, u32[]{:S(2)}) async-start(bf16[128,4,128]{2,1,0:T(4,128)(2,1)} %bitcast.27), calls=%async_computation | async-start | bytes 262144 | tf_op jit(solution)/shard_map/all_to_all | solution.py:454
  50.5 61.4 %all-to-all-start.1 = ((bf16[128,64,128]{2,1,0:T(8,128)(2,1)}), bf16[128,64,128]{2,1,0:T(8,128)(2,1)S(1)}, u32[]{:S(2)}, u32[]{:S(2)}) async-start(bf16[128,64,128]{2,1,0:T(8,128)(2,1)} %bitcast.24), calls=%async_computation.1 | async-start | bytes 4194304 | tf_op jit(solution)/shard_map/all_to_all | solution.py:459
  58.6 2.2 %copy-start = (bf16[1,8192,256]{2,1,0:T(8,128)(2,1)S(1)}, bf16[1,8192,256]{2,1,0:T(8,128)(2,1)}, u32[]{:S(2)}) copy-start(bf16[1,8192,256]{2,1,0:T(8,128)(2,1)} %param.11) | copy-start | bytes 12582916
  114.6 12.0 %collective-permute-start = (bf16[512,128]{1,0:T(8,128)(2,1)S(1)}, bf16[512,128]{1,0:T(8,128)(2,1)S(1)}, u32[]{:S(2)}, u32[]{:S(2)}) collective-permute-start(bf16[512,128]{1,0:T(8,128)(2,1)S(1)} %spectra_travel.1), channel_id=1, source_target_pairs={{0,127},{1,126},{2,125},{3,124},{4,123},{5,122},{6,121},{7,120},{8... | collective-permute-start | bytes 393224 | tf_op jit(solution)/shard_map/ppermute | solution.py:467

commit v7 on v5

--- a/solution.py
+++ b/solution.py
@@ -228,14 +228,15 @@
 
 
 def send_kernel(
-    height, plan_ref, given_ref, legendre_hbm, send_hbm,
+    height, orders_ref, given_ref, legendre_hbm, send_hbm,
     given32_ref, operand_ref, held_ref, legendre_ref, send_ref, sems, send_sems,
 ):
     for part in range(sems.shape[0]):
         legendre_read(legendre_hbm, legendre_ref, sems, part).start()
     cycles = given_ref.shape[0] // 4
     degrees = legendre_ref.shape[0]
-    order = plan_ref[0]
+    lane = lax.broadcasted_iota(jnp.int32, orders_ref.shape, 1)
+    order = jnp.sum(jnp.where(lane == lax.axis_index(BAND_SUB), orders_ref[...], 0))
     given32_ref[...] = given_ref[...].astype(jnp.float32)
     make_operands(given32_ref, operand_ref)
     alm_products(degrees - order, legendre_hbm, legendre_ref, operand_ref, held_ref, 32, height, sems)
@@ -267,13 +268,13 @@
         pltpu.make_async_copy(send_ref.at[place], send_hbm.at[place], send_sems.at[piece]).wait()
 
 
-def rows_to_send(plan, given, legendre, height=512):
+def rows_to_send(low_orders, given, legendre, height=512):
     degrees, inner = legendre.shape
     columns = given.shape[1]
     return pl.pallas_call(
         functools.partial(send_kernel, height),
         out_shape=jax.ShapeDtypeStruct((degrees, columns), jnp.bfloat16),
-        in_specs=[SMEM_SPEC, VMEM_SPEC, HBM_SPEC],
+        in_specs=[VMEM_SPEC, VMEM_SPEC, HBM_SPEC],
         out_specs=HBM_SPEC,
         scratch_shapes=[
             pltpu.VMEM(given.shape, jnp.float32),
@@ -286,7 +287,7 @@
         ],
         compiler_params=pltpu.CompilerParams(vmem_limit_bytes=SEND_VMEM),
         name="rows_to_send",
-    )(plan, given, legendre)
+    )(low_orders, given, legendre)
 
 
 def alm_kernel(
@@ -475,7 +476,7 @@
         outgoing.reshape(devices, 4, columns), BAND_SUB, split_axis=0, concat_axis=0, tiled=True
     ).reshape(4 * devices, columns)
     plan = plan_of(device_index[None], low_orders, range_rows)
-    send = rows_to_send(plan, received, legendre[0])
+    send = rows_to_send(low_orders[None], received, legendre[0])
     incoming = lax.all_to_all(
         send.reshape(devices, range_rows, columns), BAND_SUB, split_axis=0, concat_axis=0, tiled=True
     ).reshape(-1, columns)

time: 128 us -> 127 us (level)
  blocking collectives: 0 us -> 38.4 us
  starting transfers between devices: 34.7 us -> 8.26 us
  waiting for transfers between devices: 66.8 us -> 55 us
    all_to_all x0 -> x1, blocking collectives: none -> 38.4 us  [local(): lax.all_to_all(outgoing.reshape(devices, 4, columns), BAND_SUB, split_axi...]
    all_to_all x1 -> x0, starting transfers between devices: 26.4 us -> none  [local(): lax.all_to_all(outgoing.reshape(devices, 4, columns), BAND_SUB, split_axi...]
    all_to_all x1 -> x0, waiting for transfers between devices: 10.6 us -> none  [local(): lax.all_to_all(outgoing.reshape(devices, 4, columns), BAND_SUB, split_axi...]
  transfers between devices with their start and end apart: 3 -> 2, of which waited for: 3 -> 2; matrix products, arithmetic and copies ran while one was open for 0% -> 0% of each run, Pallas kernels for 6% -> 6%
where the time goes in v7:
time: 127 us
  waiting for transfers between devices  55 us (43%)
  blocking collectives  38.4 us (30%)
  Pallas kernels  20.3 us (16%)
  starting transfers between devices  8.26 us (7%)
  local copies, waits for them, and re-layouts  2.19 us (2%)
  between operations  2.02 us (2%)
    all_to_all x1, waiting for transfers between devices, local(): lax.all_to_all(send.reshape(devices, range_rows, columns), BAND_SUB, spli...  45.9 us
    all_to_all x1, blocking collectives, local(): lax.all_to_all(outgoing.reshape(devices, 4, columns), BAND_SUB, split_axi...  38.4 us
    ppermute x1, waiting for transfers between devices, local(): swapped = lax.ppermute(moving, BAND_SUB, route)  9.13 us
    all_to_all x1, starting transfers between devices, local(): lax.all_to_all(send.reshape(devices, range_rows, columns), BAND_SUB, spli...  8.12 us
    pallas_call x2, Pallas kernels, spectra_rows(): pl.pallas_call(functools.partial(spectra_kernel, travels, degrees), out_s...  5.44 us
    pallas_call x1, Pallas kernels, rows_to_send(): pl.pallas_call(functools.partial(send_kernel, height), out_shape=jax.Shap...  5.28 us
    pallas_call x1, Pallas kernels, fourier(): pl.pallas_call(functools.partial(fourier_kernel, degrees), out_shape=jax....  4.35 us
    pallas_call x1, Pallas kernels, packed_alm(): pl.pallas_call(functools.partial(alm_kernel, height), out_shape=(jax.Shap...  4.08 us
  transfers between devices with their start and end apart: 2, of which 2 were waited for; matrix products, arithmetic and copies ran while one was open for 0% of the time, Pallas kernels for 6%

profile of v7, /device:TPU:514, one launch (start us, length us, event | category | flops | bytes accessed | tf_op | source)
XLA Modules:
  0.0 127.0 jit_solution(8408924380872709573)
XLA Ops:
  0.6 0.0 copy-start.1
  1.9 4.4 %fourier.1 = bf16[512,128]{1,0:T(8,128)(2,1)} custom-call(s32[1]{0:T(128)S(6)} %copy.10.count_ref, s32[1]{0:T(128)S(6)} %copy.11.offset_ref, s32[1,128]{1,0:T(1,128)} %bitcast.20, f32[1,16384]{1,0:T(1,128)} %mask_hbm.1, bf16[64,16384]{1,0:T(8,128)(2,1)} %bitcast.25), custom_call_target="tpu_custom_call" | custom-call | tf_op jit(solution)/shard_map/fourier/pallas_call | solution.py:149
  6.3 38.4 %all_to_all.10 = bf16[128,4,128]{2,1,0:T(4,128)(2,1)S(1)} all-to-all(bf16[128,4,128]{2,1,0:T(4,128)(2,1)} %bitcast.26), channel_id=1, replica_groups=mesh['groups'=2,'band_0'=8,'band_1'=8,'sub'=2] {'band_0','band_1','sub'}, dimensions={0} | all-to-all | bytes 262144 | tf_op jit(solution)/shard_map/all_to_all | solution.py:475
  44.8 0.0 copy-done.1
  44.8 5.3 %rows_to_send.1 = bf16[8192,128]{1,0:T(8,128)(2,1)} custom-call(s32[1,128]{1,0:T(1,128)S(1)} %bitcast.21, bf16[512,128]{1,0:T(8,128)(2,1)S(1)} %bitcast.18, bf16[8192,256]{1,0:T(8,128)(2,1)} %bitcast.16), custom_call_target="tpu_custom_call" | custom-call | tf_op jit(solution)/shard_map/rows_to_send/pallas_call | solution.py:274
  50.0 8.1 %all-to-all-start.1 = ((bf16[128,64,128]{2,1,0:T(8,128)(2,1)}), bf16[128,64,128]{2,1,0:T(8,128)(2,1)S(1)}, u32[]{:S(2)}, u32[]{:S(2)}) async-start(bf16[128,64,128]{2,1,0:T(8,128)(2,1)} %bitcast.24), calls=%async_computation.1 | async-start | bytes 4194304 | tf_op jit(solution)/shard_map/all_to_all | solution.py:480
  58.2 1.1 plan.1.plan_ref
  59.3 0.0 copy-start
  59.3 2.2 %copy-done = bf16[1,8192,256]{2,1,0:T(8,128)(2,1)S(1)} copy-done((bf16[1,8192,256]{2,1,0:T(8,128)(2,1)S(1)}, bf16[1,8192,256]{2,1,0:T(8,128)(2,1)}, u32[]{:S(2)}) %copy-start) | copy-done | bytes 4194328
  61.5 4.1 %packed_alm.1 = (f32[8192,128]{1,0:T(8,128)}, f32[1,128]{1,0:T(1,128)S(1)}) custom-call(s32[3]{0:T(128)S(1)} %plan.1.plan_ref, bf16[512,128]{1,0:T(8,128)(2,1)S(1)} %bitcast.19, bf16[8192,256]{1,0:T(8,128)(2,1)S(1)} %bitcast.17), custom_call_target="tpu_custom_call" | custom-call | tf_op jit(solution)/shard_map/packed_alm/pallas_call | solution.py:314
  65.6 45.9 %all-to-all-done.1 = bf16[128,64,128]{2,1,0:T(8,128)(2,1)S(1)} async-done(((bf16[128,64,128]{2,1,0:T(8,128)(2,1)}), bf16[128,64,128]{2,1,0:T(8,128)(2,1)S(1)}, u32[]{:S(2)}, u32[]{:S(2)}) %all-to-all-start.1) | async-done | bytes 2097184 | tf_op jit(solution)/shard_map/all_to_all | solution.py:480
  111.5 2.7 %spectra_travel.1 = bf16[512,128]{1,0:T(8,128)(2,1)S(1)} custom-call(s32[3]{0:T(128)S(1)} %plan.1.plan_ref, s32[128]{0:T(128)S(1)} %copy-done.1, s32[1,128]{1,0:T(1,128)S(1)} %bitcast.22, f32[1,128]{1,0:T(1,128)S(1)} %get-tuple-element.5.weight_ref, bf16[8192,128]{1,0:T(8,128)(2,1)S(1)} %bitcast.14), custom_call_target="tpu_custom_call" | custom-call | tf_op jit(solution)/shard_map/spectra_travel/pallas_call | solution.py:442
  114.2 0.1 collective-permute-start
  114.3 2.7 %spectra_stay.1 = f32[1024,128]{1,0:T(8,128)} custom-call(s32[3]{0:T(128)S(1)} %plan.1.plan_ref, s32[128]{0:T(128)S(1)} %copy-done.1, s32[1,128]{1,0:T(1,128)S(1)} %bitcast.23, f32[1,128]{1,0:T(1,128)S(1)} %get-tuple-element.5.weight_ref, bf16[8192,128]{1,0:T(8,128)(2,1)S(1)} %bitcast.15), custom_call_target="tpu_custom_call" | custom-call | tf_op jit(solution)/shard_map/spectra_stay/pallas_call | solution.py:442
  117.1 9.1 %collective-permute-done = bf16[512,128]{1,0:T(8,128)(2,1)S(1)} collective-permute-done((bf16[512,128]{1,0:T(8,128)(2,1)S(1)}, bf16[512,128]{1,0:T(8,128)(2,1)S(1)}, u32[]{:S(2)}, u32[]{:S(2)}) %collective-permute-start) | collective-permute-done | bytes 131104 | tf_op jit(solution)/shard_map/ppermute | solution.py:486
  126.2 0.7 convert_dynamic-update-slice_fusion
Async XLA Ops:
  0.6 44.1 %copy-start.1 = (s32[128]{0:T(128)S(1)}, s32[128]{0:T(128)}, u32[]{:S(2)}) copy-start(s32[128]{0:T(128)} %order_ref.3) | copy-start | bytes 1540
  50.0 61.5 %all-to-all-start.1 = ((bf16[128,64,128]{2,1,0:T(8,128)(2,1)}), bf16[128,64,128]{2,1,0:T(8,128)(2,1)S(1)}, u32[]{:S(2)}, u32[]{:S(2)}) async-start(bf16[128,64,128]{2,1,0:T(8,128)(2,1)} %bitcast.24), calls=%async_computation.1 | async-start | bytes 4194304 | tf_op jit(solution)/shard_map/all_to_all | solution.py:480
  59.3 2.2 %copy-start = (bf16[1,8192,256]{2,1,0:T(8,128)(2,1)S(1)}, bf16[1,8192,256]{2,1,0:T(8,128)(2,1)}, u32[]{:S(2)}) copy-start(bf16[1,8192,256]{2,1,0:T(8,128)(2,1)} %param.11) | copy-start | bytes 12582916
  114.2 12.0 %collective-permute-start = (bf16[512,128]{1,0:T(8,128)(2,1)S(1)}, bf16[512,128]{1,0:T(8,128)(2,1)S(1)}, u32[]{:S(2)}, u32[]{:S(2)}) collective-permute-start(bf16[512,128]{1,0:T(8,128)(2,1)S(1)} %spectra_travel.1), channel_id=1, source_target_pairs={{0,127},{1,126},{2,125},{3,124},{4,123},{5,122},{6,121},{7,120},{8... | collective-permute-start | bytes 393224 | tf_op jit(solution)/shard_map/ppermute | solution.py:486
